TPU v7x, 128 devices: a whole 4x4x4 slice. The times are simulated.
128 devices in a mesh: seq: 32 (over z, x, core), mp: 4 (over y).
Axes of the slice: x: 4, y: 4, z: 4, core: 2. Of those that a mesh axis runs over, the one named last changes fastest.
Arguments:
- teacher_query: bfloat16 [5120, 8192], P('seq', 'mp'), may hold values from -37 to 37
- teacher_keys: bfloat16 [5120, 1024], P('seq', 'mp'), may hold values from -4 to 4
- teacher_values: bfloat16 [5120, 1024], P('seq', 'mp'), may hold values from -4 to 4
- teacher_docs: int32 [16], replicated, may hold values from 1 to 3840, 5120 in all
- student_query: bfloat16 [5120, 3584], P('seq', 'mp'), may hold values from -37 to 37
- student_keys: bfloat16 [5120, 512], P('seq', 'mp'), may hold values from -4 to 4
- student_values: bfloat16 [5120, 512], P('seq', 'mp'), may hold values from -4 to 4
- student_docs: int32 [16], replicated, may hold values from 1 to 3840, 5120 in all
- projector: bfloat16 [8192, 3584], P('mp'), may hold values from -0.125 to 0.125
- teacher_spans: int32 [32, 2, 128], P('seq'), may hold values from 0 to 159, as said below
- student_spans: int32 [32, 2, 128], P('seq'), may hold values from 0 to 159, as said below
Outputs:
- grad_query: bfloat16 [5120, 3584], P('seq', 'mp')
- grad_keys: bfloat16 [5120, 512], P('seq', 'mp')
- grad_values: bfloat16 [5120, 512], P('seq', 'mp')
Inputs may be any that keep to these rules, and one draw needn't show every extreme that they name: `teacher_spans`: column d * 4 + c of row r holds, first, the first teacher position of a span (counted within the 160 positions of index r along seq) and, second, its number of positions; it is the c-th span that index r sends to index d. A count of 0 marks an empty slot; the live slots of one destination come first; live spans cover 1 to 4 positions inside the index's positions and may intersect. One source sends at most 4 spans to one destination, and in every draw some destination receives 4 from every source. `student_spans`: column r * 4 + c of row d holds the student range (first position within the 160 positions of index d along seq, then the number of positions) of the span in column d * 4 + c of row r of teacher_spans; the count is 0 exactly where that teacher slot is empty, else 1 to 4. Ranges may intersect.
All inputs are finite; a program needn't handle non-finite values.
Results may differ from a plain program's by a relative error of at most 0.015.
Values may be sent and summed in bfloat16 or wider, within the bound.
A program may use at most 128 MiB of HBM per device.

v0:
```python
import functools

import jax
import jax.numpy as jnp
from jax import lax
from jax.experimental import pallas as pl
from jax.experimental.pallas import tpu as pltpu
from jax.sharding import PartitionSpec as P

HD = 128
ROWS = 160
SEQ = 32
TOKENS = ROWS * SEQ
SLOTS = 128
TG, TR = 2, 8
SR = 7
KV = 2 * TG * HD + 2 * HD
MESH = pl.DeviceIdType.MESH
SCALE = HD**-0.5
EXP2_SCALE = SCALE * 1.4426950408889634
LOW = -1e30
MASKED = -3e38
NDOCS = 16
ONES, FLAG = NDOCS, NDOCS + 3
FAR = 1 << 20
FB = 512
BB = 512
CHUNK = 1280
VMEM_ALL = 60 * 1024 * 1024

NT = (((1,), (1,)), ((), ()))
TN = (((0,), (0,)), ((), ()))


def dot(a, b, dims=None):
    if dims is None:
        dims = (((1,), (0,)), ((), ()))
    return lax.dot_general(a, b, dims, preferred_element_type=jnp.float32)


def place():
    me = lax.axis_index("seq")
    return me, me // 8, (me // 2) % 4, me % 2


def seq_of(z, x, c):
    return (z * 4 + x) * 2 + c


def greet(peers):
    barrier = pltpu.get_barrier_semaphore()
    for peer in peers:
        pl.semaphore_signal(barrier, inc=1, device_id=peer, device_id_type=MESH)
    pl.semaphore_wait(barrier, len(peers))


GATHER_OPS = 71


def gather_kernel(tk, tv, sk, sv, gath, own_sem, send_sem, recv_sem):
    me, z, x, c = place()
    y = lax.axis_index("mp")

    locals_ = []
    at = 0
    for i, ref in enumerate((tk, tv, sk, sv)):
        width = ref.shape[1]
        copy = pltpu.make_async_copy(
            ref, gath.at[me, :, pl.ds(at, width)], own_sem.at[i]
        )
        copy.start()
        locals_.append(copy)
        at += width

    def node(half, p, q):
        zz, xx = (q, p) if half == 0 else (p, q)
        return seq_of(lax.rem(zz + 4, 4), lax.rem(xx + 4, 4), c)

    pos = ((x, z), (z, x))
    partner = seq_of(z, x, 1 - c)
    greet(
        [(node(0, x + 1, z), y), (node(0, x + 3, z), y)]
        + [(node(0, x, z + 1), y), (node(0, x, z + 3), y)]
        + [(partner, y)]
    )

    count = [0]
    started = []

    def send(slot, rows, cols, peer):
        i = count[0]
        count[0] += 1
        ref = gath.at[slot, pl.ds(*rows), pl.ds(*cols)]
        copy = pltpu.make_async_remote_copy(
            src_ref=ref,
            dst_ref=ref,
            send_sem=send_sem.at[i],
            recv_sem=recv_sem.at[i],
            device_id=(peer, y),
            device_id_type=MESH,
        )
        copy.start()
        started.append(copy)
        return i

    def arrive(i, slot, rows, cols):
        ref = gath.at[slot, pl.ds(*rows), pl.ds(*cols)]
        pltpu.make_async_remote_copy(
            src_ref=ref,
            dst_ref=ref,
            send_sem=send_sem.at[i],
            recv_sem=recv_sem.at[i],
            device_id=(partner, y),
            device_id_type=MESH,
        ).wait_recv()

    half_rows = ((0, ROWS // 2), (ROWS // 2, ROWS // 2))
    whole, left, right = (0, KV), (0, KV // 2), (KV // 2, KV // 2)
    died = []

    def die(slot_offset, rows):
        slot, theirs = slot_offset
        died.append((send(slot, rows, whole, partner), theirs, rows))

    def both_cores(half, dp, dq):
        p, q = pos[half]
        zz, xx = (q + dq, p + dp) if half == 0 else (p + dp, q + dq)
        zz, xx = lax.rem(zz + 4, 4), lax.rem(xx + 4, 4)
        return seq_of(zz, xx, c), seq_of(zz, xx, 1 - c)

    def mine(half, dp, dq):
        return both_cores(half, dp, dq)[0]

    def peer(half, dp, dq):
        return mine(half, dp, dq)

    for copy in locals_:
        copy.wait()

    first = {}
    second = {}
    for half in (0, 1):
        rows = half_rows[half]
        for d in (1, -1):
            first[half, d] = send(me, rows, whole, peer(half, d, 0))
    for half in (0, 1):
        rows = half_rows[half]
        for d in (1, -1):
            second[half, 0, d] = send(me, rows, whole, peer(half, 0, d))
    died.append((send(me, (0, ROWS), whole, partner), partner, (0, ROWS)))

    def spread(half, dp):
        rows = half_rows[half]
        for d in (1, -1):
            second[half, dp, d] = send(mine(half, dp, 0), rows, whole, peer(half, 0, d))
        die(both_cores(half, dp, 0), rows)

    across = {}
    for d, cols in ((1, left), (-1, right)):
        for half in (0, 1):
            rows = half_rows[half]
            arrive(first[half, d], mine(half, -d, 0), rows, whole)
            across[half, d] = send(mine(half, -d, 0), rows, cols, peer(half, d, 0))
            spread(half, -d)

    further = {}

    def pass_on(half, dp):
        rows = half_rows[half]
        for d, cols in ((1, left), (-1, right)):
            slot = mine(half, dp, -d)
            arrive(second[half, dp, d], slot, rows, whole)
            further[half, dp, d] = send(slot, rows, cols, peer(half, 0, d))
            die(both_cores(half, dp, -d), rows)

    for half in (0, 1):
        pass_on(half, 0)
    for half in (0, 1):
        rows = half_rows[half]
        for d, cols in ((1, left), (-1, right)):
            arrive(across[half, d], mine(half, -2 * d, 0), rows, cols)
        spread(half, 2)
    for dp in (-1, 1):
        for half in (0, 1):
            pass_on(half, dp)

    def ended(half, dp):
        rows = half_rows[half]
        for d, cols in ((1, left), (-1, right)):
            arrive(further[half, dp, d], mine(half, dp, -2 * d), rows, cols)
        die(both_cores(half, dp, 2), rows)

    for half in (0, 1):
        ended(half, 0)
    for half in (0, 1):
        pass_on(half, 2)
    for dp in (-1, 1, 2):
        for half in (0, 1):
            ended(half, dp)
    for i, slot, rows in died:
        arrive(i, slot, rows, whole)
    for copy in started:
        copy.wait_send()
    assert count[0] == GATHER_OPS, count[0]


def gather(tk, tv, sk, sv):
    hbm = pl.BlockSpec(memory_space=pl.ANY)
    return pl.pallas_call(
        gather_kernel,
        out_shape=jax.ShapeDtypeStruct((SEQ, ROWS, KV), jnp.bfloat16),
        in_specs=[hbm] * 4,
        out_specs=pl.BlockSpec(memory_space=pltpu.VMEM),
        scratch_shapes=[
            pltpu.SemaphoreType.DMA((4,)),
            pltpu.SemaphoreType.DMA((GATHER_OPS,)),
            pltpu.SemaphoreType.DMA((GATHER_OPS,)),
        ],
        compiler_params=pltpu.CompilerParams(
            collective_id=0, has_side_effects=True, vmem_limit_bytes=VMEM_ALL
        ),
        name="gather",
    )(tk, tv, sk, sv)


def doc_lanes(docs_ref):
    lane = lax.broadcasted_iota(jnp.int32, (1, 128), 1)
    first = jnp.where((lane >= ONES) & (lane < FLAG), -1, FAR)
    last = jnp.full((1, 128), FAR, jnp.int32)
    bound = jnp.int32(0)
    for k in range(NDOCS):
        first = jnp.where(lane == k, bound, first)
        bound = bound + docs_ref[k]
        last = jnp.where(lane == k, bound, last)
    return lane, first, last


def first_start(docs_ref, place_):
    bound = jnp.int32(0)
    lo = jnp.int32(0)
    for k in range(NDOCS):
        bound = bound + docs_ref[k]
        lo = jnp.where(bound <= place_, bound, lo)
    return lo


def key_marks(at, count, limit, lanes):
    lane, first, last = lanes
    first = jnp.where(lane == FLAG, limit, first)
    places = at + lax.broadcasted_iota(jnp.int32, (count, 128), 0)
    inside = (places >= first) & (places < last)
    return inside.astype(jnp.float32).astype(jnp.bfloat16)


def stack_heads(dst, src, first_head, ratio):
    for h in range(ratio):
        cols = slice((first_head + h) * HD, (first_head + h + 1) * HD)
        dst[h * 128 : (h + 1) * 128, 0:HD] = src[0:128, cols]
        dst[ratio * 128 + h * 32 : ratio * 128 + (h + 1) * 32, 0:HD] = src[128:160, cols]


def parts(value):
    high = value.astype(jnp.bfloat16).astype(jnp.float32)
    rest = value - high
    middle = rest.astype(jnp.bfloat16).astype(jnp.float32)
    return high, middle, rest - middle


def query_marks(places, shift, lanes):
    lane, first, last = lanes
    inside = (places >= first) & (places < last)
    marks = jnp.where((lane < NDOCS) & jnp.logical_not(inside) | (lane == FLAG), LOW, 0.0)
    for k, part in enumerate(parts(-shift)):
        marks = jnp.where(lane == ONES + k, part, marks)
    return marks.astype(jnp.bfloat16)


def mark_queries(dst, keys, place_, lanes, ratio):
    for begin, count, base in ((0, 128, 0), (128, 32, ratio * 128)):
        own = keys[begin : begin + count, :].astype(jnp.float32)
        places = place_ + begin + lax.broadcasted_iota(jnp.int32, (count, 1), 0)
        for h in range(ratio):
            rows = slice(base + h * count, base + (h + 1) * count)
            q = dst[rows, 0:HD].astype(jnp.float32)
            shift = jnp.sum(q * own, axis=1, keepdims=True)
            dst[rows, HD:] = query_marks(places, shift, lanes)


def lane_rows(ratio):
    lane = lax.broadcasted_iota(jnp.int32, (1, ratio * ROWS), 1)
    cut = ratio * 128
    return jnp.where(lane < cut, lane & 127, 128 + ((lane - cut) & 31))


def chunks(width):
    return [(a, min(a + CHUNK, width)) for a in range(0, width, CHUNK)]


def own_pairs(a, b, lanes_row):
    return lax.broadcasted_iota(jnp.int32, (ROWS, b - a), 0) <= lanes_row[:, a:b]


class Window:
    def __init__(self, docs_ref, gath, first_col, own, blocks, own_sem, sems, size):
        self.place = lax.axis_index("seq") * ROWS
        self.lo = first_start(docs_ref, self.place)
        self.size = size
        self.gath, self.own, self.blocks = gath, own, blocks
        self.own_sem, self.sems = own_sem, sems
        self.cols = pl.ds(first_col, own.shape[1])
        self.steps = (jnp.maximum(self.place - self.lo, 0) + size - 1) // size
        self.lanes = doc_lanes(docs_ref)

    def at(self, step):
        return pl.multiple_of(jnp.maximum(self.place - (step + 1) * self.size, 0), 16)

    def own_copy(self):
        rows = pl.ds(pl.multiple_of(self.place, 16), ROWS)
        return pltpu.make_async_copy(self.gath.at[rows, self.cols], self.own, self.own_sem)

    def copy(self, step):
        rows = pl.ds(self.at(step), self.size)
        return pltpu.make_async_copy(
            self.gath.at[rows, self.cols], self.blocks.at[step], self.sems.at[step]
        )

    def start(self):
        self.own_copy().start()

        @pl.loop(0, self.steps)
        def _(step):
            self.copy(step).start()

    def marks(self, step):
        return key_marks(
            self.at(step), self.size, self.place - step * self.size, self.lanes
        )

    def own_marks(self):
        return key_marks(self.place, ROWS, jnp.int32(FAR), self.lanes)


def extended(values):
    ones = jnp.ones((16, values.shape[0]), jnp.bfloat16)
    return jnp.concatenate([jnp.transpose(values), ones], axis=0)


def attend(window, q_refs, l_ref, acc_ref, top_ref, ratio):
    groups = len(q_refs)
    width = ratio * ROWS
    lanes_row = lane_rows(ratio)
    top_ref[...] = jnp.zeros(top_ref.shape, jnp.float32)

    def scores(g, keys, a, b, own):
        s = dot(keys, q_refs[g][a:b, :], NT)
        return jnp.where(own_pairs(a, b, lanes_row), s, MASKED) if own else s

    def block(kv, marks, own):
        for g in range(groups):
            keys = jnp.concatenate([kv[:, g * HD : (g + 1) * HD], marks], axis=1)
            values_t = extended(kv[:, (groups + g) * HD : (groups + g + 1) * HD])
            for a, b in chunks(width):
                p = jnp.exp2(scores(g, keys, a, b, own) * EXP2_SCALE)
                add = dot(values_t, p.astype(jnp.bfloat16))
                if l_ref is not None:
                    total = jnp.sum(p.reshape(p.shape[0] // 8, 8, b - a), axis=0)
                    l_ref[g, :, a:b] = total if own else l_ref[g, :, a:b] + total
                acc_ref[g, :, a:b] = add if own else acc_ref[g, :, a:b] + add

    def safe_block(kv, marks, own):
        for g in range(groups):
            keys = jnp.concatenate([kv[:, g * HD : (g + 1) * HD], marks], axis=1)
            values_t = extended(kv[:, (groups + g) * HD : (groups + g + 1) * HD])
            for a, b in chunks(width):
                s = scores(g, keys, a, b, own)
                old = jnp.full((1, b - a), LOW) if own else top_ref[g, :, a:b]
                new = jnp.maximum(old, jnp.max(s, axis=0, keepdims=True))
                p = jnp.exp2((s - new) * EXP2_SCALE)
                add = dot(values_t, p.astype(jnp.bfloat16))
                top_ref[g, :, a:b] = new
                alpha = None if own else jnp.exp2((old - new) * EXP2_SCALE)
                if l_ref is not None:
                    total = jnp.sum(p.reshape(p.shape[0] // 8, 8, b - a), axis=0)
                    l_ref[g, :, a:b] = total if own else l_ref[g, :, a:b] * alpha + total
                acc_ref[g, :, a:b] = add if own else acc_ref[g, :, a:b] * alpha + add

    block(window.own, window.own_marks(), True)

    @pl.loop(0, window.steps)
    def _(step):
        window.copy(step).wait()
        block(window.blocks.at[step], window.marks(step), False)

    @pl.when(jnp.logical_not(jnp.max(acc_ref[:, HD : HD + 8, :]) < 2.0**100))
    def _():
        safe_block(window.own, window.own_marks(), True)

        @pl.loop(0, window.steps)
        def _(step):
            safe_block(window.blocks.at[step], window.marks(step), False)


def member_rows(spans_ref):
    start = spans_ref[0, 0:1, :]
    length = spans_ref[0, 1:2, :]
    row = lax.broadcasted_iota(jnp.int32, (ROWS, SLOTS), 0)
    inside = (row >= start) & (row < start + length)
    weight = 1.0 / jnp.maximum(length, 1).astype(jnp.float32)
    return inside.astype(jnp.float32), weight, length


def forward_kernel(
    tdocs, sdocs, tq, sq, gath, tspans, pooled, sctx, qback,
    tstack, sstack, town, sown, tblocks, sblocks, tacc, ttop, sl, sacc, stop,
    own_sem, tsem, ssem,
):
    tcols, scols = 2 * TG * HD, 2 * HD
    twin = Window(tdocs, gath, 0, town, tblocks, own_sem.at[0], tsem, FB)
    swin = Window(sdocs, gath, tcols, sown, sblocks, own_sem.at[1], ssem, FB)
    twin.start()
    swin.start()
    for g in range(TG):
        stack_heads(tstack.at[g], tq, g * TR, TR)
    stack_heads(sstack, sq, 0, SR)
    twin.own_copy().wait()
    for g in range(TG):
        mark_queries(
            tstack.at[g], town.at[:, g * HD : (g + 1) * HD], twin.place, twin.lanes, TR
        )
    swin.own_copy().wait()
    mark_queries(sstack, sown.at[:, 0:HD], swin.place, swin.lanes, SR)

    attend(twin, [tstack.at[g] for g in range(TG)], None, tacc, ttop, TR)
    attend(swin, [sstack], sl, sacc, stop, SR)

    member, weight, _ = member_rows(tspans)
    member = member.astype(jnp.bfloat16)
    tail = jnp.concatenate([member[128:160]] * TR, axis=0)
    owner = lax.broadcasted_iota(jnp.int32, (TR * 32, SLOTS), 0) // 32
    for g in range(TG):
        inverse = 1.0 / tacc[g, HD : HD + 1]
        context_t = (tacc[g, 0:HD] * inverse).astype(jnp.bfloat16)
        for h in range(TR):
            sums = dot(context_t[:, h * 128 : (h + 1) * 128], member[0:128]) + dot(
                context_t[:, TR * 128 :], jnp.where(owner == h, tail, jnp.zeros_like(tail))
            )
            cols = slice((g * TR + h) * HD, (g * TR + h + 1) * HD)
            pooled[:, cols] = jnp.transpose(sums * weight).astype(jnp.bfloat16)

    total = jnp.sum(sl[0], axis=0, keepdims=True)
    inverse = 1.0 / sacc[0, HD : HD + 1]
    extra = stop[0] + jnp.log2(total) * (1.0 / EXP2_SCALE)
    for h in range(SR):
        cols = slice(h * 128, (h + 1) * 128)
        sctx[0:128, cols] = jnp.transpose(sacc[0, 0:HD, cols] * inverse[:, cols]).astype(
            jnp.bfloat16
        )
    rest = jnp.transpose(sacc[0, 0:HD, SR * 128 :] * inverse[:, SR * 128 :]).astype(jnp.bfloat16)
    for h in range(SR):
        sctx[128:160, h * HD : (h + 1) * HD] = rest[h * 32 : (h + 1) * 32]
    qback[:, 0:HD] = sstack[:, 0:HD]
    lane = swin.lanes[0]
    for a in range(0, SR * ROWS, 128):
        b = min(a + 128, SR * ROWS)
        column = jnp.transpose(jnp.broadcast_to(extra[:, a:b], (8, b - a)))[:, 0:1]
        marks = sstack[a:b, HD:].astype(jnp.float32)
        ones = (lane >= ONES) & (lane < FLAG)
        before = jnp.sum(jnp.where(ones, marks, 0.0), axis=1, keepdims=True)
        for k, part in enumerate(parts(before - column)):
            marks = jnp.where(lane == ONES + k, part, marks)
        qback[a:b, HD:] = marks.astype(jnp.bfloat16)


def forward(tdocs, sdocs, tq, sq, gath, tspans):
    vmem = pl.BlockSpec(memory_space=pltpu.VMEM)
    smem = pl.BlockSpec(memory_space=pltpu.SMEM)
    hbm = pl.BlockSpec(memory_space=pl.ANY)
    tw, sw = TR * ROWS, SR * ROWS
    bf16, f32 = jnp.bfloat16, jnp.float32
    return pl.pallas_call(
        forward_kernel,
        out_shape=(
            jax.ShapeDtypeStruct((SLOTS, TG * TR * HD), bf16),
            jax.ShapeDtypeStruct((ROWS, SR * HD), bf16),
            jax.ShapeDtypeStruct((sw, 2 * HD), bf16),
        ),
        in_specs=[smem, smem, vmem, vmem, hbm, vmem],
        out_specs=(vmem, vmem, vmem),
        scratch_shapes=[
            pltpu.VMEM((TG, tw, 2 * HD), bf16),
            pltpu.VMEM((sw, 2 * HD), bf16),
            pltpu.VMEM((ROWS, 2 * TG * HD), bf16),
            pltpu.VMEM((ROWS, 2 * HD), bf16),
            pltpu.VMEM((TOKENS // FB, FB, 2 * TG * HD), bf16),
            pltpu.VMEM((TOKENS // FB, FB, 2 * HD), bf16),
            pltpu.VMEM((TG, HD + 16, tw), f32),
            pltpu.VMEM((TG, 1, tw), f32),
            pltpu.VMEM((1, 8, sw), f32),
            pltpu.VMEM((1, HD + 16, sw), f32),
            pltpu.VMEM((1, 1, sw), f32),
            pltpu.SemaphoreType.DMA((2,)),
            pltpu.SemaphoreType.DMA((TOKENS // FB,)),
            pltpu.SemaphoreType.DMA((TOKENS // FB,)),
        ],
        compiler_params=pltpu.CompilerParams(vmem_limit_bytes=VMEM_ALL),
        name="forward",
    )(tdocs, sdocs, tq, sq, gath, tspans)


def align_kernel(
    pooled, projector, arrived, wide, part, near, far, blocks, landed,
    load_sem, send_sem, recv_sem, a2a_send, a2a_recv, own_sem,
):
    me = lax.axis_index("seq")
    y = lax.axis_index("mp")
    cols = part.shape[2]
    half = SLOTS // 2
    up, down, across = lax.rem(y + 1, 4), lax.rem(y + 3, 4), lax.rem(y + 2, 4)
    order = (across, up, down, y)
    loads = []
    for i, target in enumerate(order):
        begin = pl.multiple_of(target * cols, 128)
        copy = pltpu.make_async_copy(
            projector.at[:, pl.ds(begin, cols)], wide.at[i], load_sem.at[i]
        )
        copy.start()
        loads.append(copy)

    barrier = pltpu.get_barrier_semaphore()
    for target in (up, down):
        pl.semaphore_signal(barrier, inc=1, device_id=(me, target), device_id_type=MESH)

    @pl.loop(1, SEQ)
    def _(k):
        pl.semaphore_signal(
            barrier, inc=1, device_id=(lax.rem(me + k, SEQ), y), device_id_type=MESH
        )

    pl.semaphore_wait(barrier, SEQ + 1)

    def project(i):
        loads[i].wait()
        return dot(pooled[...], wide[i])

    def remote(i, src, dst, target):
        return pltpu.make_async_remote_copy(
            src_ref=src,
            dst_ref=dst,
            send_sem=send_sem.at[i],
            recv_sem=recv_sem.at[i],
            device_id=(me, target),
            device_id_type=MESH,
        )

    low, high = pl.ds(0, half), pl.ds(half, half)
    hops = [
        remote(0, part.at[0, low], far.at[0], up),
        remote(1, part.at[0, high], far.at[1], down),
        remote(2, part.at[1, high], near.at[0, high], up),
        remote(3, part.at[2, low], near.at[1, low], down),
        remote(4, part.at[1, low], near.at[0, low], up),
        remote(5, part.at[2, high], near.at[1, high], down),
    ]
    part[0] = project(0).astype(jnp.bfloat16)
    hops[0].start()
    hops[1].start()
    for_up = project(1)
    part[1, half:] = for_up[half:].astype(jnp.bfloat16)
    hops[2].start()
    for_down = project(2)
    part[2, :half] = for_down[:half].astype(jnp.bfloat16)
    hops[3].start()
    hops[0].wait_recv()
    part[1, :half] = (for_up[:half] + far[0].astype(jnp.float32)).astype(jnp.bfloat16)
    hops[4].start()
    hops[1].wait_recv()
    part[2, half:] = (for_down[half:] + far[1].astype(jnp.float32)).astype(jnp.bfloat16)
    hops[5].start()
    mine = project(3)
    for i in (2, 3, 4, 5):
        hops[i].wait_recv()
    total = mine + near[0].astype(jnp.float32) + near[1].astype(jnp.float32)
    for d in range(SEQ):
        blocks[d] = total[4 * d : 4 * d + 4].astype(jnp.bfloat16)

    def exchange(k, src, target):
        return pltpu.make_async_remote_copy(
            src_ref=blocks.at[target],
            dst_ref=landed.at[src],
            send_sem=a2a_send.at[k],
            recv_sem=a2a_recv.at[k],
            device_id=(target, y),
            device_id_type=MESH,
        )

    @pl.loop(1, SEQ)
    def _(k):
        exchange(k, me, lax.rem(me + k, SEQ)).start()

    own = pltpu.make_async_copy(blocks.at[me], landed.at[me], own_sem)
    own.start()
    own.wait()

    @pl.loop(1, SEQ)
    def _(k):
        exchange(k, lax.rem(me + SEQ - k, SEQ), lax.rem(me + k, SEQ)).wait_recv()

    for s in range(SEQ):
        arrived[4 * s : 4 * s + 4, :] = landed[s].astype(jnp.float32)

    @pl.loop(1, SEQ)
    def _(k):
        exchange(k, me, lax.rem(me + k, SEQ)).wait_send()

    for hop in hops:
        hop.wait_send()


def align(pooled, projector):
    vmem = pl.BlockSpec(memory_space=pltpu.VMEM)
    depth, width = projector.shape
    cols = width // 4
    return pl.pallas_call(
        align_kernel,
        out_shape=jax.ShapeDtypeStruct((SLOTS, cols), jnp.float32),
        in_specs=[vmem, pl.BlockSpec(memory_space=pl.ANY)],
        out_specs=vmem,
        scratch_shapes=[
            pltpu.VMEM((4, depth, cols), jnp.bfloat16),
            pltpu.VMEM((3, SLOTS, cols), jnp.bfloat16),
            pltpu.VMEM((2, SLOTS, cols), jnp.bfloat16),
            pltpu.VMEM((2, SLOTS // 2, cols), jnp.bfloat16),
            pltpu.VMEM((SEQ, 4, cols), jnp.bfloat16),
            pltpu.VMEM((SEQ, 4, cols), jnp.bfloat16),
            pltpu.SemaphoreType.DMA((4,)),
            pltpu.SemaphoreType.DMA((6,)),
            pltpu.SemaphoreType.DMA((6,)),
            pltpu.SemaphoreType.DMA((SEQ,)),
            pltpu.SemaphoreType.DMA((SEQ,)),
            pltpu.SemaphoreType.DMA,
        ],
        compiler_params=pltpu.CompilerParams(
            collective_id=1, has_side_effects=True, vmem_limit_bytes=VMEM_ALL
        ),
        name="align",
    )(pooled, projector)


def backward_kernel(
    sdocs, qback, gath, sctx, arrived, sspans, grad_q, terms,
    dstack, dq_t, own, blocks, own_sem, sem,
):
    window = Window(sdocs, gath, 2 * TG * HD, own, blocks, own_sem, sem, BB)
    window.start()
    width = SR * ROWS
    terms[...] = jnp.zeros(terms.shape, terms.dtype)
    member, weight, length = member_rows(sspans)
    columns = jnp.transpose(
        jnp.concatenate(
            [weight, (length > 0).astype(jnp.float32), jnp.zeros((6, SLOTS), jnp.float32)],
            axis=0,
        )
    )
    weight, live = columns[:, 0:1], columns[:, 1:2]
    member_t = jnp.transpose(member).astype(jnp.bfloat16)
    member = member.astype(jnp.bfloat16)
    pooled = dot(member_t, sctx[...]) * weight
    gap = jnp.where(live > 0.0, pooled - arrived[...], 0.0) * weight
    high = gap.astype(jnp.bfloat16)
    low = (gap - high.astype(jnp.float32)).astype(jnp.bfloat16)
    dout = (dot(member, high) + dot(member, low)).astype(jnp.bfloat16)
    lane = window.lanes[0]
    for h in range(SR):
        cols = slice(h * HD, (h + 1) * HD)
        head = dout[:, cols]
        delta = jnp.sum(
            head.astype(jnp.float32) * sctx[:, cols].astype(jnp.float32), axis=1, keepdims=True
        )
        marks = jnp.zeros((ROWS, 128), jnp.float32)
        for k, part in enumerate(parts(-delta)):
            marks = jnp.where(lane == ONES + k, part, marks)
        marks = marks.astype(jnp.bfloat16)
        top = slice(h * 128, (h + 1) * 128)
        rest = slice(SR * 128 + h * 32, SR * 128 + (h + 1) * 32)
        dstack[top, 0:HD] = head[0:128]
        dstack[rest, 0:HD] = head[128:160]
        dstack[top, HD:] = marks[0:128]
        dstack[rest, HD:] = marks[128:160]

    lanes_row = lane_rows(SR)

    def block(kv, marks, at, own_rows):
        count = kv.shape[0]
        rows = pl.ds(at, count)
        plain = kv[:, 0:HD]
        keys = jnp.concatenate([plain, marks], axis=1)
        values = jnp.concatenate([kv[:, HD:], marks], axis=1)
        keys_t = jnp.transpose(plain)
        grad_k = jnp.zeros((count, HD), jnp.float32)
        grad_v = jnp.zeros((count, HD), jnp.float32)
        for a, b in chunks(width):
            p = jnp.exp2(dot(keys, qback[a:b, :], NT) * EXP2_SCALE)
            if own_rows:
                p = jnp.where(own_pairs(a, b, lanes_row), p, 0.0)
            ds = (p * dot(values, dstack[a:b, :], NT)).astype(jnp.bfloat16)
            grad_v = grad_v + dot(p.astype(jnp.bfloat16), dstack[a:b, 0:HD])
            grad_k = grad_k + dot(ds, qback[a:b, 0:HD])
            add = dot(keys_t, ds)
            if own_rows:
                dq_t[:, a:b] = add
            else:
                dq_t[:, a:b] += add
        grad = jnp.concatenate([grad_k * SCALE, grad_v], axis=1)
        if not own_rows:
            grad = grad + terms[rows, :].astype(jnp.float32)
        terms[rows, :] = grad.astype(jnp.bfloat16)

    window.own_copy().wait()
    block(window.own, window.own_marks(), pl.multiple_of(window.place, 16), True)

    @pl.loop(0, window.steps)
    def _(step):
        window.copy(step).wait()
        block(window.blocks.at[step], window.marks(step), window.at(step), False)

    for h in range(SR):
        cols = slice(h * HD, (h + 1) * HD)
        grad_q[0:128, cols] = (jnp.transpose(dq_t[:, h * 128 : (h + 1) * 128]) * SCALE).astype(
            jnp.bfloat16
        )
    rest = (jnp.transpose(dq_t[:, SR * 128 :]) * SCALE).astype(jnp.bfloat16)
    for h in range(SR):
        grad_q[128:160, h * HD : (h + 1) * HD] = rest[h * 32 : (h + 1) * 32]


def backward(sdocs, qback, gath, sctx, arrived, sspans):
    vmem = pl.BlockSpec(memory_space=pltpu.VMEM)
    smem = pl.BlockSpec(memory_space=pltpu.SMEM)
    hbm = pl.BlockSpec(memory_space=pl.ANY)
    sw = SR * ROWS
    bf16 = jnp.bfloat16
    return pl.pallas_call(
        backward_kernel,
        out_shape=(
            jax.ShapeDtypeStruct((ROWS, SR * HD), bf16),
            jax.ShapeDtypeStruct((TOKENS, 2 * HD), bf16),
        ),
        in_specs=[smem, vmem, hbm, vmem, vmem, vmem],
        out_specs=(vmem, vmem),
        scratch_shapes=[
            pltpu.VMEM((sw, 2 * HD), bf16),
            pltpu.VMEM((HD, sw), jnp.float32),
            pltpu.VMEM((ROWS, 2 * HD), bf16),
            pltpu.VMEM((TOKENS // BB, BB, 2 * HD), bf16),
            pltpu.SemaphoreType.DMA,
            pltpu.SemaphoreType.DMA((TOKENS // BB,)),
        ],
        compiler_params=pltpu.CompilerParams(vmem_limit_bytes=VMEM_ALL),
        name="backward",
    )(sdocs, qback, gath, sctx, arrived, sspans)


def scatter_kernel(
    terms, grad_k, grad_v, theirs, chip, far1, near1, out1, far2, near2,
    die_send, die_recv, send_sem, recv_sem,
):
    me, z, x, c = place()
    y = lax.axis_index("mp")
    partner = seq_of(z, x, 1 - c)
    wrap = lambda v: lax.rem(v + 4, 4)

    def peer(axis, d):
        return seq_of(wrap(z + d), x, c) if axis == "z" else seq_of(z, wrap(x + d), c)

    greet(
        [(peer("z", 1), y), (peer("z", 3), y), (peer("x", 1), y), (peer("x", 3), y)]
        + [(partner, y)]
    )

    def crossing(i):
        return pltpu.make_async_remote_copy(
            src_ref=terms.at[pl.ds(4 * i, 4), 1 - c],
            dst_ref=theirs.at[pl.ds(4 * i, 4)],
            send_sem=die_send.at[i],
            recv_sem=die_recv.at[i],
            device_id=(partner, y),
            device_id_type=MESH,
        )

    for i in range(4):
        crossing(i).start()

    def remote(i, src, dst, target):
        return pltpu.make_async_remote_copy(
            src_ref=src,
            dst_ref=dst,
            send_sem=send_sem.at[i],
            recv_sem=recv_sem.at[i],
            device_id=(target, y),
            device_id_type=MESH,
        )

    for i in range(4):
        crossing(i).wait_recv()
        part = pl.ds(4 * i, 4)
        both = terms[part, c].astype(jnp.float32) + theirs[part].astype(jnp.float32)
        low = both.astype(jnp.bfloat16)
        chip[0, i] = low[:, 0:80]
        for j in range(4):
            chip[1, j, i] = low[j, 80:160]

    f32 = lambda v: v.astype(jnp.float32)
    all_hops = []
    axes = (("z", "x"), ("x", "z"))
    pos = ((z, x), (x, z))
    first = []
    for h in (0, 1):
        axis = axes[h][0]
        p = pos[h][0]
        up, down = peer(axis, 1), peer(axis, 3)
        to_far, to_up, to_down = wrap(p + 2), wrap(p + 1), wrap(p + 3)
        lo, hi = pl.ds(0, 2), pl.ds(2, 2)
        hops = [
            remote(12 * h + 0, chip.at[h, to_far, lo], far1.at[h, 0], up),
            remote(12 * h + 1, chip.at[h, to_far, hi], far1.at[h, 1], down),
            remote(12 * h + 2, chip.at[h, to_up, hi], near1.at[h, 0, hi], up),
            remote(12 * h + 3, chip.at[h, to_down, lo], near1.at[h, 1, lo], down),
            remote(12 * h + 4, chip.at[h, to_up, lo], near1.at[h, 0, lo], up),
            remote(12 * h + 5, chip.at[h, to_down, hi], near1.at[h, 1, hi], down),
        ]
        for k in range(4):
            hops[k].start()
        first.append((hops, to_up, to_down))
        all_hops += hops
    for h in (0, 1):
        hops, to_up, to_down = first[h]
        lo, hi = pl.ds(0, 2), pl.ds(2, 2)
        hops[0].wait_recv()
        chip[h, to_up, lo] = (f32(chip[h, to_up, lo]) + f32(far1[h, 0])).astype(jnp.bfloat16)
        hops[4].start()
        hops[1].wait_recv()
        chip[h, to_down, hi] = (f32(chip[h, to_down, hi]) + f32(far1[h, 1])).astype(jnp.bfloat16)
        hops[5].start()
    second = []
    for h in (0, 1):
        hops = first[h][0]
        for k in range(2, 6):
            hops[k].wait_recv()
        out1[h] = (f32(chip[h, pos[h][0]]) + f32(near1[h, 0]) + f32(near1[h, 1])).astype(
            jnp.bfloat16
        )
        axis = axes[h][1]
        p = pos[h][1]
        up, down = peer(axis, 1), peer(axis, 3)
        to_far, to_up, to_down = wrap(p + 2), wrap(p + 1), wrap(p + 3)
        lo, hi = pl.ds(0, HD), pl.ds(HD, HD)
        rows = pl.ds(0, 80)
        hops = [
            remote(12 * h + 6, out1.at[h, to_far, rows, lo], far2.at[h, 0], up),
            remote(12 * h + 7, out1.at[h, to_far, rows, hi], far2.at[h, 1], down),
            remote(12 * h + 8, out1.at[h, to_up, rows, hi], near2.at[h, 0, rows, hi], up),
            remote(12 * h + 9, out1.at[h, to_down, rows, lo], near2.at[h, 1, rows, lo], down),
            remote(12 * h + 10, out1.at[h, to_up, rows, lo], near2.at[h, 0, rows, lo], up),
            remote(12 * h + 11, out1.at[h, to_down, rows, hi], near2.at[h, 1, rows, hi], down),
        ]
        for k in range(4):
            hops[k].start()
        second.append((hops, to_up, to_down))
        all_hops += hops
    for h in (0, 1):
        hops, to_up, to_down = second[h]
        hops[0].wait_recv()
        out1[h, to_up, :, 0:HD] = (f32(out1[h, to_up, :, 0:HD]) + f32(far2[h, 0])).astype(
            jnp.bfloat16
        )
        hops[4].start()
        hops[1].wait_recv()
        out1[h, to_down, :, HD:] = (f32(out1[h, to_down, :, HD:]) + f32(far2[h, 1])).astype(
            jnp.bfloat16
        )
        hops[5].start()
    for h in (0, 1):
        hops = second[h][0]
        for k in range(2, 6):
            hops[k].wait_recv()
        total = (
            f32(out1[h, pos[h][1]]) + f32(near2[h, 0]) + f32(near2[h, 1])
        ).astype(jnp.bfloat16)
        grad_k[80 * h : 80 * h + 80, :] = total[:, 0:HD]
        grad_v[80 * h : 80 * h + 80, :] = total[:, HD:]
    for hop in all_hops:
        hop.wait_send()
    for i in range(4):
        crossing(i).wait_send()


def scatter(terms):
    vmem = pl.BlockSpec(memory_space=pltpu.VMEM)
    bf16 = jnp.bfloat16
    width = terms.shape[-1]
    return pl.pallas_call(
        scatter_kernel,
        out_shape=(
            jax.ShapeDtypeStruct((ROWS, HD), bf16),
            jax.ShapeDtypeStruct((ROWS, HD), bf16),
        ),
        in_specs=[vmem],
        out_specs=(vmem, vmem),
        scratch_shapes=[
            pltpu.VMEM((16, ROWS, width), bf16),
            pltpu.VMEM((2, 4, 4, 80, width), bf16),
            pltpu.VMEM((2, 2, 2, 80, width), bf16),
            pltpu.VMEM((2, 2, 4, 80, width), bf16),
            pltpu.VMEM((2, 4, 80, width), bf16),
            pltpu.VMEM((2, 2, 80, HD), bf16),
            pltpu.VMEM((2, 2, 80, width), bf16),
            pltpu.SemaphoreType.DMA((4,)),
            pltpu.SemaphoreType.DMA((4,)),
            pltpu.SemaphoreType.DMA((24,)),
            pltpu.SemaphoreType.DMA((24,)),
        ],
        compiler_params=pltpu.CompilerParams(
            collective_id=2, has_side_effects=True, vmem_limit_bytes=VMEM_ALL
        ),
        name="scatter",
    )(terms)


def body(
    teacher_query,
    teacher_keys,
    teacher_values,
    teacher_docs,
    student_query,
    student_keys,
    student_values,
    student_docs,
    projector,
    teacher_spans,
    student_spans,
):
    gath = gather(teacher_keys, teacher_values, student_keys, student_values)
    gath = gath.reshape(TOKENS, KV)
    pooled, sctx, qback = forward(
        teacher_docs, student_docs, teacher_query, student_query, gath, teacher_spans
    )
    arrived = align(pooled, projector)
    grad_q, terms = backward(student_docs, qback, gath, sctx, arrived, student_spans)
    grad_k, grad_v = scatter(terms.reshape(16, 2, ROWS, 2 * HD))
    return grad_q, grad_k, grad_v


def solution(mesh):
    return jax.shard_map(
        body,
        mesh=mesh,
        in_specs=(
            P("seq", "mp"),
            P("seq", "mp"),
            P("seq", "mp"),
            P(),
            P("seq", "mp"),
            P("seq", "mp"),
            P("seq", "mp"),
            P(),
            P("mp", None),
            P("seq", None, None),
            P("seq", None, None),
        ),
        out_specs=(P("seq", "mp"), P("seq", "mp"), P("seq", "mp")),
        check_vma=False,
    )
```

profile of v0, /device:TPU:0, one launch (start us, length us, event | category | flops | bytes accessed | tf_op | source)
XLA Modules:
  0.0 125.8 jit_solution(14034187130073582944)
XLA Ops:
  0.6 33.0 %gather.1 = bf16[32,160,768]{2,1,0:T(8,128)(2,1)} custom-call(bf16[160,256]{1,0:T(8,128)(2,1)} %tk.1, bf16[160,256]{1,0:T(8,128)(2,1)} %tv.1, bf16[160,128]{1,0:T(8,128)(2,1)} %sk.1, bf16[160,128]{1,0:T(8,128)(2,1)} %sv.1), custom_call_target="tpu_custom_call" | custom-call | tf_op jit(solution)/shard_map/gather/pallas_call | solution.py:209
  33.7 6.9 %forward.1 = (bf16[128,2048]{1,0:T(8,128)(2,1)}, bf16[160,896]{1,0:T(8,128)(2,1)}, bf16[1120,256]{1,0:T(8,128)(2,1)}) custom-call(s32[16]{0:T(128)} %tdocs.1, s32[16]{0:T(128)} %sdocs.3, bf16[160,2048]{1,0:T(8,128)(2,1)} %tq.1, bf16[160,896]{1,0:T(8,128)(2,1)} %sq.1, bf16[5120,768]{1,0:T(8,128)(2,1)} %bitcast.2, s32[1,2,128]{2,1,0:T(2,128)} %tspans.1), custom_call_target="tpu_custom_call" | custom-call | tf_op jit(solution)/shard_map/forward/pallas_call | solution.py:480
  40.6 41.5 %align.1.arrived = f32[128,896]{1,0:T(8,128)} custom-call(bf16[128,2048]{1,0:T(8,128)(2,1)} %get-tuple-element.12.pooled, bf16[2048,3584]{1,0:T(8,128)(2,1)} %projector.1), custom_call_target="tpu_custom_call" | custom-call | tf_op jit(solution)/shard_map/align/pallas_call | solution.py:623
  82.1 4.7 %backward.1 = (bf16[160,896]{1,0:T(8,128)(2,1)}, bf16[5120,256]{1,0:T(8,128)(2,1)}) custom-call(s32[16]{0:T(128)} %sdocs.3, bf16[1120,256]{1,0:T(8,128)(2,1)} %get-tuple-element.10.qback, bf16[5120,768]{1,0:T(8,128)(2,1)} %bitcast.3, bf16[160,896]{1,0:T(8,128)(2,1)} %get-tuple-element.11.sctx, f32[128,896]{1,0:T(8,128)} %align.1.arrived, s32[1,2,128]{2,1,0:T(2,128)} %sspans.1), custom_call_target="tpu_custom_call" | custom-call | tf_op jit(solution)/shard_map/backward/pallas_call | solution.py:742
  86.8 36.1 %scatter.1 = (bf16[160,128]{1,0:T(8,128)(2,1)}, bf16[160,128]{1,0:T(8,128)(2,1)}) custom-call(bf16[16,2,160,256]{3,2,1,0:T(8,128)(2,1)} %bitcast.4), custom_call_target="tpu_custom_call" | custom-call | tf_op jit(solution)/shard_map/scatter/pallas_call | solution.py:901
  123.0 1.4 %copy.16 = bf16[160,128]{1,0:T(8,128)(2,1)} copy(bf16[160,128]{1,0:T(8,128)(2,1)} %get-tuple-element.21) | data formatting | bytes 81920
  124.4 1.4 %copy.17 = bf16[160,128]{1,0:T(8,128)(2,1)} copy(bf16[160,128]{1,0:T(8,128)(2,1)} %get-tuple-element.22) | data formatting | bytes 81920
where the time goes:
time: 125 us; the launch traced here: 126 us
  Pallas kernels  122 us (98%)
  local copies, waits for them, and re-layouts  2.8 us (2%)
    pallas_call x1, Pallas kernels, align(): pl.pallas_call(align_kernel, out_shape=jax.ShapeDtypeStruct((SLOTS, cols)...  41.5 us
    pallas_call x1, Pallas kernels, scatter(): pl.pallas_call(scatter_kernel, out_shape=(jax.ShapeDtypeStruct((ROWS, HD)...  36.1 us
    pallas_call x1, Pallas kernels, gather(): pl.pallas_call(gather_kernel, out_shape=jax.ShapeDtypeStruct((SEQ, ROWS,...  33 us
    pallas_call x1, Pallas kernels, forward(): pl.pallas_call(forward_kernel, out_shape=(jax.ShapeDtypeStruct((SLOTS, TG...  6.95 us
    pallas_call x1, Pallas kernels, backward(): pl.pallas_call(backward_kernel, out_shape=(jax.ShapeDtypeStruct((ROWS, SR...  4.68 us
    unnamed x2, local copies, waits for them, and re-layouts  2.8 us

commit v1 on v0

v1 whole, which is shorter than its diff:
```python
import functools

import jax
import jax.numpy as jnp
from jax import lax
from jax.experimental import pallas as pl
from jax.experimental.pallas import tpu as pltpu
from jax.sharding import PartitionSpec as P

HD = 128
ROWS = 160
SEQ = 32
TOKENS = ROWS * SEQ
SLOTS = 128
TG, TR = 2, 8
SR = 7
MESH = pl.DeviceIdType.MESH
SCALE = HD**-0.5
EXP2_SCALE = SCALE * 1.4426950408889634
LOW = -1e30
MASKED = -3e38
NDOCS = 16
ONES, FLAG = NDOCS, NDOCS + 3
FAR = 1 << 20
FB = 512
BB = 512
SB = 640
TKV, SKV = 2 * TG * HD, 2 * HD
CHUNK = 1280
VMEM_ALL = 60 * 1024 * 1024

NT = (((1,), (1,)), ((), ()))
TN = (((0,), (0,)), ((), ()))


def dot(a, b, dims=None):
    if dims is None:
        dims = (((1,), (0,)), ((), ()))
    return lax.dot_general(a, b, dims, preferred_element_type=jnp.float32)


def place():
    me = lax.axis_index("seq")
    return me, me // 8, (me // 2) % 4, me % 2


def seq_of(z, x, c):
    return (z * 4 + x) * 2 + c


def greet(peers):
    barrier = pltpu.get_barrier_semaphore()
    for peer in peers:
        pl.semaphore_signal(barrier, inc=1, device_id=peer, device_id_type=MESH)
    pl.semaphore_wait(barrier, len(peers))


GATHER_OPS = 71


def seq_neighbours():
    me, z, x, c = place()
    wrap = lambda v: lax.rem(v + 4, 4)
    return [
        seq_of(z, wrap(x + 1), c),
        seq_of(z, wrap(x + 3), c),
        seq_of(wrap(z + 1), x, c),
        seq_of(wrap(z + 3), x, c),
        seq_of(z, x, 1 - c),
    ]


def torus_gather(buf, send_sem, recv_sem):
    me, z, x, c = place()
    y = lax.axis_index("mp")
    pos = ((x, z), (z, x))
    partner = seq_of(z, x, 1 - c)
    width = buf.shape[2]
    half_rows = ((0, ROWS // 2), (ROWS // 2, ROWS // 2))
    whole, left, right = (0, width), (0, width // 2), (width // 2, width // 2)
    ways = ((1, left), (-1, right))
    count = [0]
    started = []
    died = []

    def copy_of(i, slot, rows, cols, target):
        ref = buf.at[slot, pl.ds(*rows), pl.ds(*cols)]
        return pltpu.make_async_remote_copy(
            src_ref=ref,
            dst_ref=ref,
            send_sem=send_sem.at[i],
            recv_sem=recv_sem.at[i],
            device_id=(target, y),
            device_id_type=MESH,
        )

    def send(slot, rows, cols, target):
        i = count[0]
        count[0] += 1
        copy = copy_of(i, slot, rows, cols, target)
        copy.start()
        started.append(copy)
        return i

    def arrive(i, slot, rows, cols):
        copy_of(i, slot, rows, cols, partner).wait_recv()

    def both_cores(half, dp, dq):
        p, q = pos[half]
        zz, xx = (q + dq, p + dp) if half == 0 else (p + dp, q + dq)
        zz, xx = lax.rem(zz + 4, 4), lax.rem(xx + 4, 4)
        return seq_of(zz, xx, c), seq_of(zz, xx, 1 - c)

    def mine(half, dp, dq):
        return both_cores(half, dp, dq)[0]

    def die(slots, rows):
        slot, theirs = slots
        died.append((send(slot, rows, whole, partner), theirs, rows))

    first, second, across, further = {}, {}, {}, {}

    def spread(half, dp):
        rows = half_rows[half]
        for d in (1, -1):
            second[half, dp, d] = send(mine(half, dp, 0), rows, whole, mine(half, 0, d))
        die(both_cores(half, dp, 0), rows)

    def pass_on(half, dp):
        rows = half_rows[half]
        for d, cols in ways:
            slot = mine(half, dp, -d)
            arrive(second[half, dp, d], slot, rows, whole)
            further[half, dp, d] = send(slot, rows, cols, mine(half, 0, d))
            die(both_cores(half, dp, -d), rows)

    def ended(half, dp):
        rows = half_rows[half]
        for d, cols in ways:
            arrive(further[half, dp, d], mine(half, dp, -2 * d), rows, cols)
        die(both_cores(half, dp, 2), rows)

    for half in (0, 1):
        for d in (1, -1):
            first[half, d] = send(me, half_rows[half], whole, mine(half, d, 0))
    for half in (0, 1):
        for d in (1, -1):
            second[half, 0, d] = send(me, half_rows[half], whole, mine(half, 0, d))
    died.append((send(me, (0, ROWS), whole, partner), partner, (0, ROWS)))
    yield
    for d, cols in ways:
        for half in (0, 1):
            rows = half_rows[half]
            arrive(first[half, d], mine(half, -d, 0), rows, whole)
            across[half, d] = send(mine(half, -d, 0), rows, cols, mine(half, d, 0))
    for d in (1, -1):
        for half in (0, 1):
            spread(half, -d)
    yield
    for half in (0, 1):
        pass_on(half, 0)
    yield
    for half in (0, 1):
        for d, cols in ways:
            arrive(across[half, d], mine(half, -2 * d, 0), half_rows[half], cols)
        spread(half, 2)
    yield
    for dp in (-1, 1):
        for half in (0, 1):
            pass_on(half, dp)
    for half in (0, 1):
        ended(half, 0)
    yield
    for half in (0, 1):
        pass_on(half, 2)
    for dp in (-1, 1, 2):
        for half in (0, 1):
            ended(half, dp)
    for i, slot, rows in died:
        arrive(i, slot, rows, whole)
    yield
    for copy in started:
        copy.wait_send()
    assert count[0] == GATHER_OPS


def own_rows_in(refs, buf, sems):
    me = lax.axis_index("seq")
    copies = []
    at = 0
    for i, ref in enumerate(refs):
        width = ref.shape[1]
        copies.append(
            pltpu.make_async_copy(ref, buf.at[me, :, pl.ds(at, width)], sems.at[i])
        )
        at += width
    return copies


def doc_lanes(docs_ref):
    lane = lax.broadcasted_iota(jnp.int32, (1, 128), 1)
    first = jnp.where((lane >= ONES) & (lane < FLAG), -1, FAR)
    last = jnp.full((1, 128), FAR, jnp.int32)
    bound = jnp.int32(0)
    for k in range(NDOCS):
        first = jnp.where(lane == k, bound, first)
        bound = bound + docs_ref[k]
        last = jnp.where(lane == k, bound, last)
    return lane, first, last


def first_start(docs_ref, place_):
    bound = jnp.int32(0)
    lo = jnp.int32(0)
    for k in range(NDOCS):
        bound = bound + docs_ref[k]
        lo = jnp.where(bound <= place_, bound, lo)
    return lo


def key_marks(at, count, limit, lanes):
    lane, first, last = lanes
    first = jnp.where(lane == FLAG, limit, first)
    places = at + lax.broadcasted_iota(jnp.int32, (count, 128), 0)
    inside = (places >= first) & (places < last)
    return inside.astype(jnp.float32).astype(jnp.bfloat16)


def stack_heads(dst, src, first_head, ratio):
    for h in range(ratio):
        cols = slice((first_head + h) * HD, (first_head + h + 1) * HD)
        dst[h * 128 : (h + 1) * 128, 0:HD] = src[0:128, cols]
        dst[ratio * 128 + h * 32 : ratio * 128 + (h + 1) * 32, 0:HD] = src[128:160, cols]


def parts(value):
    high = value.astype(jnp.bfloat16).astype(jnp.float32)
    rest = value - high
    middle = rest.astype(jnp.bfloat16).astype(jnp.float32)
    return high, middle, rest - middle


def query_marks(places, shift, lanes):
    lane, first, last = lanes
    inside = (places >= first) & (places < last)
    marks = jnp.where((lane < NDOCS) & jnp.logical_not(inside) | (lane == FLAG), LOW, 0.0)
    for k, part in enumerate(parts(-shift)):
        marks = jnp.where(lane == ONES + k, part, marks)
    return marks.astype(jnp.bfloat16)


def mark_queries(dst, keys, place_, lanes, ratio):
    for begin, count, base in ((0, 128, 0), (128, 32, ratio * 128)):
        own = keys[begin : begin + count, :].astype(jnp.float32)
        places = place_ + begin + lax.broadcasted_iota(jnp.int32, (count, 1), 0)
        for h in range(ratio):
            rows = slice(base + h * count, base + (h + 1) * count)
            q = dst[rows, 0:HD].astype(jnp.float32)
            shift = jnp.sum(q * own, axis=1, keepdims=True)
            dst[rows, HD:] = query_marks(places, shift, lanes)


def lane_rows(ratio):
    lane = lax.broadcasted_iota(jnp.int32, (1, ratio * ROWS), 1)
    cut = ratio * 128
    return jnp.where(lane < cut, lane & 127, 128 + ((lane - cut) & 31))


def chunks(width):
    return [(a, min(a + CHUNK, width)) for a in range(0, width, CHUNK)]


def own_pairs(a, b, lanes_row):
    return lax.broadcasted_iota(jnp.int32, (ROWS, b - a), 0) <= lanes_row[:, a:b]


class Window:
    def __init__(self, docs_ref, gath, first_col, own, blocks, own_sem, sems, size):
        self.place = lax.axis_index("seq") * ROWS
        self.lo = first_start(docs_ref, self.place)
        self.size = size
        self.gath, self.own, self.blocks = gath, own, blocks
        self.own_sem, self.sems = own_sem, sems
        self.cols = pl.ds(first_col, own.shape[1])
        self.steps = (jnp.maximum(self.place - self.lo, 0) + size - 1) // size
        self.lanes = doc_lanes(docs_ref)

    def at(self, step):
        return pl.multiple_of(jnp.maximum(self.place - (step + 1) * self.size, 0), 16)

    def own_copy(self):
        rows = pl.ds(pl.multiple_of(self.place, 16), ROWS)
        return pltpu.make_async_copy(self.gath.at[rows, self.cols], self.own, self.own_sem)

    def copy(self, step):
        rows = pl.ds(self.at(step), self.size)
        return pltpu.make_async_copy(
            self.gath.at[rows, self.cols], self.blocks.at[step], self.sems.at[step]
        )

    def start(self):
        self.own_copy().start()

        @pl.loop(0, self.steps)
        def _(step):
            self.copy(step).start()

    def marks(self, step):
        return key_marks(
            self.at(step), self.size, self.place - step * self.size, self.lanes
        )

    def own_marks(self):
        return key_marks(self.place, ROWS, jnp.int32(FAR), self.lanes)


def extended(values):
    ones = jnp.ones((16, values.shape[0]), jnp.bfloat16)
    return jnp.concatenate([jnp.transpose(values), ones], axis=0)


class Attention:
    def __init__(self, queries, sums, acc, top, ratio):
        self.queries, self.sums, self.acc, self.top = queries, sums, acc, top
        self.lanes_row = lane_rows(ratio)
        self.chunks = chunks(ratio * ROWS)

    def pieces(self, kv, marks, own):
        groups = len(self.queries)
        for g in range(groups):
            keys = jnp.concatenate([kv[:, g * HD : (g + 1) * HD], marks], axis=1)
            values = extended(kv[:, (groups + g) * HD : (groups + g + 1) * HD])
            for a, b in self.chunks:
                s = dot(keys, self.queries[g][a:b, :], NT)
                if own:
                    s = jnp.where(own_pairs(a, b, self.lanes_row), s, MASKED)
                yield g, a, b, s, values

    def sum_rows(self, p):
        return jnp.sum(p.reshape(p.shape[0] // 8, 8, p.shape[1]), axis=0)

    def block(self, kv, marks, own):
        sums, acc = self.sums, self.acc
        if own:
            self.top[...] = jnp.zeros(self.top.shape, jnp.float32)
        for g, a, b, s, values in self.pieces(kv, marks, own):
            p = jnp.exp2(s * EXP2_SCALE)
            add = dot(values, p.astype(jnp.bfloat16))
            if sums is not None:
                total = self.sum_rows(p)
                sums[g, :, a:b] = total if own else sums[g, :, a:b] + total
            acc[g, :, a:b] = add if own else acc[g, :, a:b] + add

    def safe_block(self, kv, marks, own):
        sums, acc, top = self.sums, self.acc, self.top
        for g, a, b, s, values in self.pieces(kv, marks, own):
            old = jnp.full((1, b - a), LOW) if own else top[g, :, a:b]
            new = jnp.maximum(old, jnp.max(s, axis=0, keepdims=True))
            p = jnp.exp2((s - new) * EXP2_SCALE)
            add = dot(values, p.astype(jnp.bfloat16))
            top[g, :, a:b] = new
            alpha = None if own else jnp.exp2((old - new) * EXP2_SCALE)
            if sums is not None:
                total = self.sum_rows(p)
                sums[g, :, a:b] = total if own else sums[g, :, a:b] * alpha + total
            acc[g, :, a:b] = add if own else acc[g, :, a:b] * alpha + add

    def safe_window(self, window):
        self.safe_block(window.own, window.own_marks(), True)

        @pl.loop(0, window.steps)
        def _(step):
            self.safe_block(window.blocks.at[step], window.marks(step), False)


def too_large(weight_sums):
    return jnp.logical_not(jnp.max(weight_sums) < 2.0**100)


def member_rows(spans_ref):
    start = spans_ref[0, 0:1, :]
    length = spans_ref[0, 1:2, :]
    row = lax.broadcasted_iota(jnp.int32, (ROWS, SLOTS), 0)
    inside = (row >= start) & (row < start + length)
    weight = 1.0 / jnp.maximum(length, 1).astype(jnp.float32)
    return inside.astype(jnp.float32), weight, length


def forward_kernel(
    tdocs, tq, gath, tspans, pooled, stack, own, blocks, acc, top, own_sem, sem
):
    window = Window(tdocs, gath, 0, own, blocks, own_sem, sem, FB)
    window.start()
    for g in range(TG):
        stack_heads(stack.at[g], tq, g * TR, TR)
    window.own_copy().wait()
    for g in range(TG):
        mark_queries(
            stack.at[g], own.at[:, g * HD : (g + 1) * HD], window.place, window.lanes, TR
        )
    attention = Attention([stack.at[g] for g in range(TG)], None, acc, top, TR)
    attention.block(own, window.own_marks(), True)

    @pl.loop(0, window.steps)
    def _(step):
        window.copy(step).wait()
        attention.block(blocks.at[step], window.marks(step), False)

    @pl.when(too_large(acc[:, HD : HD + 8, :]))
    def _():
        attention.safe_window(window)

    member, weight, _ = member_rows(tspans)
    member = member.astype(jnp.bfloat16)
    tail = jnp.concatenate([member[128:160]] * TR, axis=0)
    owner = lax.broadcasted_iota(jnp.int32, (TR * 32, SLOTS), 0) // 32
    for g in range(TG):
        inverse = 1.0 / acc[g, HD : HD + 1]
        context_t = (acc[g, 0:HD] * inverse).astype(jnp.bfloat16)
        for h in range(TR):
            sums = dot(context_t[:, h * 128 : (h + 1) * 128], member[0:128]) + dot(
                context_t[:, TR * 128 :], jnp.where(owner == h, tail, jnp.zeros_like(tail))
            )
            cols = slice((g * TR + h) * HD, (g * TR + h + 1) * HD)
            pooled[:, cols] = jnp.transpose(sums * weight).astype(jnp.bfloat16)


def forward(tdocs, tq, gath, tspans):
    vmem = pl.BlockSpec(memory_space=pltpu.VMEM)
    smem = pl.BlockSpec(memory_space=pltpu.SMEM)
    hbm = pl.BlockSpec(memory_space=pl.ANY)
    tw = TR * ROWS
    bf16, f32 = jnp.bfloat16, jnp.float32
    return pl.pallas_call(
        forward_kernel,
        out_shape=jax.ShapeDtypeStruct((SLOTS, TG * TR * HD), bf16),
        in_specs=[smem, vmem, hbm, vmem],
        out_specs=vmem,
        scratch_shapes=[
            pltpu.VMEM((TG, tw, 2 * HD), bf16),
            pltpu.VMEM((ROWS, 2 * TG * HD), bf16),
            pltpu.VMEM((TOKENS // FB, FB, 2 * TG * HD), bf16),
            pltpu.VMEM((TG, HD + 16, tw), f32),
            pltpu.VMEM((TG, 1, tw), f32),
            pltpu.SemaphoreType.DMA,
            pltpu.SemaphoreType.DMA((TOKENS // FB,)),
        ],
        compiler_params=pltpu.CompilerParams(vmem_limit_bytes=VMEM_ALL),
        name="forward",
    )(tdocs, tq, gath, tspans)


def student_results(attention, stack, lanes, sctx, qback):
    acc = attention.acc
    total = jnp.sum(attention.sums[0], axis=0, keepdims=True)
    inverse = 1.0 / acc[0, HD : HD + 1]
    extra = attention.top[0] + jnp.log2(total) * (1.0 / EXP2_SCALE)
    for h in range(SR):
        cols = slice(h * 128, (h + 1) * 128)
        sctx[0:128, cols] = jnp.transpose(acc[0, 0:HD, cols] * inverse[:, cols]).astype(
            jnp.bfloat16
        )
    rest = jnp.transpose(acc[0, 0:HD, SR * 128 :] * inverse[:, SR * 128 :]).astype(jnp.bfloat16)
    for h in range(SR):
        sctx[128:160, h * HD : (h + 1) * HD] = rest[h * 32 : (h + 1) * 32]
    qback[:, 0:HD] = stack[:, 0:HD]
    lane = lanes[0]
    ones = (lane >= ONES) & (lane < FLAG)
    for a in range(0, SR * ROWS, 128):
        b = min(a + 128, SR * ROWS)
        column = jnp.transpose(jnp.broadcast_to(extra[:, a:b], (8, b - a)))[:, 0:1]
        marks = stack[a:b, HD:].astype(jnp.float32)
        before = jnp.sum(jnp.where(ones, marks, 0.0), axis=1, keepdims=True)
        for k, part in enumerate(parts(before - column)):
            marks = jnp.where(lane == ONES + k, part, marks)
        qback[a:b, HD:] = marks.astype(jnp.bfloat16)


def gather_kernel(tk, tv, sk, sv, gath, own_sem, send_sem, recv_sem):
    y = lax.axis_index("mp")
    copies = own_rows_in((tk, tv, sk, sv), gath, own_sem)
    for copy in copies:
        copy.start()
    greet([(peer, y) for peer in seq_neighbours()])
    for copy in copies:
        copy.wait()
    for _ in torus_gather(gath, send_sem, recv_sem):
        pass


def gather(tk, tv, sk, sv):
    hbm = pl.BlockSpec(memory_space=pl.ANY)
    return pl.pallas_call(
        gather_kernel,
        out_shape=jax.ShapeDtypeStruct((SEQ, ROWS, TKV + SKV), jnp.bfloat16),
        in_specs=[hbm] * 4,
        out_specs=pl.BlockSpec(memory_space=pltpu.VMEM),
        scratch_shapes=[
            pltpu.SemaphoreType.DMA((4,)),
            pltpu.SemaphoreType.DMA((GATHER_OPS,)),
            pltpu.SemaphoreType.DMA((GATHER_OPS,)),
        ],
        compiler_params=pltpu.CompilerParams(
            collective_id=0, has_side_effects=True, vmem_limit_bytes=VMEM_ALL
        ),
        name="gather",
    )(tk, tv, sk, sv)


def align_kernel(
    sdocs, pooled, projector, gath, sk, sv, sq, arrived, sctx, qback, weight_sums,
    wide, part, near, far, blocks, landed, kv, stack, sums, acc, top,
    load_sem, send_sem, recv_sem, a2a_send, a2a_recv, own_sem,
):
    me = lax.axis_index("seq")
    y = lax.axis_index("mp")
    cols = part.shape[2]
    half = SLOTS // 2
    up, down, across = lax.rem(y + 1, 4), lax.rem(y + 3, 4), lax.rem(y + 2, 4)
    order = (across, up, down, y)
    loads = []
    for i, target in enumerate(order):
        begin = pl.multiple_of(target * cols, 128)
        copy = pltpu.make_async_copy(
            projector.at[:, pl.ds(begin, cols)], wide.at[i], load_sem.at[i]
        )
        copy.start()
        loads.append(copy)
    student = pltpu.make_async_copy(gath.at[:, pl.ds(TKV, SKV)], kv, own_sem.at[1])
    student.start()

    barrier = pltpu.get_barrier_semaphore()
    for target in (up, down):
        pl.semaphore_signal(barrier, inc=1, device_id=(me, target), device_id_type=MESH)

    @pl.loop(1, SEQ)
    def _(k):
        pl.semaphore_signal(
            barrier, inc=1, device_id=(lax.rem(me + k, SEQ), y), device_id_type=MESH
        )

    pl.semaphore_wait(barrier, SEQ + 1)

    def project(i):
        loads[i].wait()
        return dot(pooled[...], wide[i])

    def remote(i, src, dst, target):
        return pltpu.make_async_remote_copy(
            src_ref=src,
            dst_ref=dst,
            send_sem=send_sem.at[i],
            recv_sem=recv_sem.at[i],
            device_id=(me, target),
            device_id_type=MESH,
        )

    low, high = pl.ds(0, half), pl.ds(half, half)
    hops = [
        remote(0, part.at[0, low], far.at[0], up),
        remote(1, part.at[0, high], far.at[1], down),
        remote(2, part.at[1, high], near.at[0, high], up),
        remote(3, part.at[2, low], near.at[1, low], down),
        remote(4, part.at[1, low], near.at[0, low], up),
        remote(5, part.at[2, high], near.at[1, high], down),
    ]
    part[0] = project(0).astype(jnp.bfloat16)
    hops[0].start()
    hops[1].start()
    for_up = project(1)
    part[1, half:] = for_up[half:].astype(jnp.bfloat16)
    hops[2].start()
    for_down = project(2)
    part[2, :half] = for_down[:half].astype(jnp.bfloat16)
    hops[3].start()
    place_ = me * ROWS
    lanes = doc_lanes(sdocs)
    stack_heads(stack, sq, 0, SR)
    mark_queries(stack, sk[...], place_, lanes, SR)
    attention = Attention([stack], sums, acc, top, SR)
    attention.block(
        jnp.concatenate([sk[...], sv[...]], axis=1),
        key_marks(place_, ROWS, jnp.int32(FAR), lanes),
        True,
    )
    count = (place_ + SB - 1) // SB

    def student_blocks(first, last):
        @pl.loop(first, last)
        def _(b):
            rows = pl.ds(pl.multiple_of(b * SB, SB), SB)
            attention.block(kv[rows], key_marks(b * SB, SB, place_, lanes), False)

    student.wait()
    hops[0].wait_recv()
    part[1, :half] = (for_up[:half] + far[0].astype(jnp.float32)).astype(jnp.bfloat16)
    hops[4].start()
    hops[1].wait_recv()
    part[2, half:] = (for_down[half:] + far[1].astype(jnp.float32)).astype(jnp.bfloat16)
    hops[5].start()
    mine = project(3)
    student_blocks(0, count // 2)
    for i in (2, 3, 4, 5):
        hops[i].wait_recv()
    total = mine + near[0].astype(jnp.float32) + near[1].astype(jnp.float32)
    for d in range(SEQ):
        blocks[d] = total[4 * d : 4 * d + 4].astype(jnp.bfloat16)

    def exchange(k, src, target):
        return pltpu.make_async_remote_copy(
            src_ref=blocks.at[target],
            dst_ref=landed.at[src],
            send_sem=a2a_send.at[k],
            recv_sem=a2a_recv.at[k],
            device_id=(target, y),
            device_id_type=MESH,
        )

    @pl.loop(1, SEQ)
    def _(k):
        exchange(k, me, lax.rem(me + k, SEQ)).start()

    own = pltpu.make_async_copy(blocks.at[me], landed.at[me], own_sem.at[0])
    own.start()
    student_blocks(count // 2, count)
    weight_sums[...] = acc[0, HD : HD + 8, :]
    student_results(attention, stack, lanes, sctx, qback)
    own.wait()

    @pl.loop(1, SEQ)
    def _(k):
        exchange(k, lax.rem(me + SEQ - k, SEQ), lax.rem(me + k, SEQ)).wait_recv()

    for s in range(SEQ):
        arrived[4 * s : 4 * s + 4, :] = landed[s].astype(jnp.float32)

    @pl.loop(1, SEQ)
    def _(k):
        exchange(k, me, lax.rem(me + k, SEQ)).wait_send()

    for hop in hops:
        hop.wait_send()


def align(sdocs, pooled, projector, gath, sk, sv, sq):
    vmem = pl.BlockSpec(memory_space=pltpu.VMEM)
    smem = pl.BlockSpec(memory_space=pltpu.SMEM)
    hbm = pl.BlockSpec(memory_space=pl.ANY)
    depth, width = projector.shape
    cols = width // 4
    sw = SR * ROWS
    bf16, f32 = jnp.bfloat16, jnp.float32
    return pl.pallas_call(
        align_kernel,
        out_shape=(
            jax.ShapeDtypeStruct((SLOTS, cols), f32),
            jax.ShapeDtypeStruct((ROWS, SR * HD), bf16),
            jax.ShapeDtypeStruct((sw, 2 * HD), bf16),
            jax.ShapeDtypeStruct((8, sw), f32),
        ),
        in_specs=[smem, vmem, hbm, hbm, vmem, vmem, vmem],
        out_specs=(vmem,) * 4,
        scratch_shapes=[
            pltpu.VMEM((4, depth, cols), bf16),
            pltpu.VMEM((3, SLOTS, cols), bf16),
            pltpu.VMEM((2, SLOTS, cols), bf16),
            pltpu.VMEM((2, SLOTS // 2, cols), bf16),
            pltpu.VMEM((SEQ, 4, cols), bf16),
            pltpu.VMEM((SEQ, 4, cols), bf16),
            pltpu.VMEM((TOKENS, SKV), bf16),
            pltpu.VMEM((sw, 2 * HD), bf16),
            pltpu.VMEM((1, 8, sw), f32),
            pltpu.VMEM((1, HD + 16, sw), f32),
            pltpu.VMEM((1, 1, sw), f32),
            pltpu.SemaphoreType.DMA((4,)),
            pltpu.SemaphoreType.DMA((6,)),
            pltpu.SemaphoreType.DMA((6,)),
            pltpu.SemaphoreType.DMA((SEQ,)),
            pltpu.SemaphoreType.DMA((SEQ,)),
            pltpu.SemaphoreType.DMA((2,)),
        ],
        compiler_params=pltpu.CompilerParams(
            collective_id=1, has_side_effects=True, vmem_limit_bytes=VMEM_ALL
        ),
        name="align",
    )(sdocs, pooled, projector, gath, sk, sv, sq)


def backward_kernel(
    sdocs, qback_in, gath, sctx_in, weight_sums, sq, arrived, sspans, grad_q, terms,
    dstack, dq_t, own, blocks, qback, sctx, stack, sums, acc, top, own_sem, sem,
):
    window = Window(sdocs, gath, TKV, own, blocks, own_sem, sem, BB)
    window.start()
    qback[...] = qback_in[...]
    sctx[...] = sctx_in[...]
    window.own_copy().wait()

    @pl.loop(0, window.steps)
    def _(step):
        window.copy(step).wait()

    @pl.when(too_large(weight_sums[...]))
    def _():
        stack_heads(stack, sq, 0, SR)
        mark_queries(stack, own.at[:, 0:HD], window.place, window.lanes, SR)
        attention = Attention([stack], sums, acc, top, SR)
        attention.safe_window(window)
        student_results(attention, stack, window.lanes, sctx, qback)

    width = SR * ROWS
    terms[...] = jnp.zeros(terms.shape, terms.dtype)
    member, weight, length = member_rows(sspans)
    columns = jnp.transpose(
        jnp.concatenate(
            [weight, (length > 0).astype(jnp.float32), jnp.zeros((6, SLOTS), jnp.float32)],
            axis=0,
        )
    )
    weight, live = columns[:, 0:1], columns[:, 1:2]
    member_t = jnp.transpose(member).astype(jnp.bfloat16)
    member = member.astype(jnp.bfloat16)
    pooled = dot(member_t, sctx[...]) * weight
    gap = jnp.where(live > 0.0, pooled - arrived[...], 0.0) * weight
    high = gap.astype(jnp.bfloat16)
    low = (gap - high.astype(jnp.float32)).astype(jnp.bfloat16)
    dout = (dot(member, high) + dot(member, low)).astype(jnp.bfloat16)
    lane = window.lanes[0]
    for h in range(SR):
        cols = slice(h * HD, (h + 1) * HD)
        head = dout[:, cols]
        delta = jnp.sum(
            head.astype(jnp.float32) * sctx[:, cols].astype(jnp.float32), axis=1, keepdims=True
        )
        marks = jnp.zeros((ROWS, 128), jnp.float32)
        for k, part in enumerate(parts(-delta)):
            marks = jnp.where(lane == ONES + k, part, marks)
        marks = marks.astype(jnp.bfloat16)
        top = slice(h * 128, (h + 1) * 128)
        rest = slice(SR * 128 + h * 32, SR * 128 + (h + 1) * 32)
        dstack[top, 0:HD] = head[0:128]
        dstack[rest, 0:HD] = head[128:160]
        dstack[top, HD:] = marks[0:128]
        dstack[rest, HD:] = marks[128:160]

    lanes_row = lane_rows(SR)

    def block(kv, marks, at, own_rows):
        count = kv.shape[0]
        rows = pl.ds(at, count)
        plain = kv[:, 0:HD]
        keys = jnp.concatenate([plain, marks], axis=1)
        values = jnp.concatenate([kv[:, HD:], marks], axis=1)
        keys_t = jnp.transpose(plain)
        grad_k = jnp.zeros((count, HD), jnp.float32)
        grad_v = jnp.zeros((count, HD), jnp.float32)
        for a, b in chunks(width):
            p = jnp.exp2(dot(keys, qback[a:b, :], NT) * EXP2_SCALE)
            if own_rows:
                p = jnp.where(own_pairs(a, b, lanes_row), p, 0.0)
            ds = (p * dot(values, dstack[a:b, :], NT)).astype(jnp.bfloat16)
            grad_v = grad_v + dot(p.astype(jnp.bfloat16), dstack[a:b, 0:HD])
            grad_k = grad_k + dot(ds, qback[a:b, 0:HD])
            add = dot(keys_t, ds)
            if own_rows:
                dq_t[:, a:b] = add
            else:
                dq_t[:, a:b] += add
        grad = jnp.concatenate([grad_k * SCALE, grad_v], axis=1)
        if not own_rows:
            grad = grad + terms[rows, :].astype(jnp.float32)
        terms[rows, :] = grad.astype(jnp.bfloat16)

    block(window.own, window.own_marks(), pl.multiple_of(window.place, 16), True)

    @pl.loop(0, window.steps)
    def _(step):
        block(window.blocks.at[step], window.marks(step), window.at(step), False)

    for h in range(SR):
        cols = slice(h * HD, (h + 1) * HD)
        grad_q[0:128, cols] = (jnp.transpose(dq_t[:, h * 128 : (h + 1) * 128]) * SCALE).astype(
            jnp.bfloat16
        )
    rest = (jnp.transpose(dq_t[:, SR * 128 :]) * SCALE).astype(jnp.bfloat16)
    for h in range(SR):
        grad_q[128:160, h * HD : (h + 1) * HD] = rest[h * 32 : (h + 1) * 32]


def backward(sdocs, qback, gath, sctx, weight_sums, sq, arrived, sspans):
    vmem = pl.BlockSpec(memory_space=pltpu.VMEM)
    smem = pl.BlockSpec(memory_space=pltpu.SMEM)
    hbm = pl.BlockSpec(memory_space=pl.ANY)
    sw = SR * ROWS
    bf16 = jnp.bfloat16
    return pl.pallas_call(
        backward_kernel,
        out_shape=(
            jax.ShapeDtypeStruct((ROWS, SR * HD), bf16),
            jax.ShapeDtypeStruct((TOKENS, 2 * HD), bf16),
        ),
        in_specs=[smem, vmem, hbm, vmem, vmem, vmem, vmem, vmem],
        out_specs=(vmem, vmem),
        scratch_shapes=[
            pltpu.VMEM((sw, 2 * HD), bf16),
            pltpu.VMEM((HD, sw), jnp.float32),
            pltpu.VMEM((ROWS, 2 * HD), bf16),
            pltpu.VMEM((TOKENS // BB, BB, 2 * HD), bf16),
            pltpu.VMEM((sw, 2 * HD), bf16),
            pltpu.VMEM((ROWS, SR * HD), bf16),
            pltpu.VMEM((sw, 2 * HD), bf16),
            pltpu.VMEM((1, 8, sw), jnp.float32),
            pltpu.VMEM((1, HD + 16, sw), jnp.float32),
            pltpu.VMEM((1, 1, sw), jnp.float32),
            pltpu.SemaphoreType.DMA,
            pltpu.SemaphoreType.DMA((TOKENS // BB,)),
        ],
        compiler_params=pltpu.CompilerParams(vmem_limit_bytes=VMEM_ALL),
        name="backward",
    )(sdocs, qback, gath, sctx, weight_sums, sq, arrived, sspans)


def scatter_kernel(
    terms, pieces, theirs, chip, far1, near1, out1, far2,
    die_send, die_recv, send_sem, recv_sem,
):
    me, z, x, c = place()
    y = lax.axis_index("mp")
    partner = seq_of(z, x, 1 - c)
    wrap = lambda v: lax.rem(v + 4, 4)

    def peer(axis, d):
        return seq_of(wrap(z + d), x, c) if axis == "z" else seq_of(z, wrap(x + d), c)

    greet(
        [(peer("z", 1), y), (peer("z", 3), y), (peer("x", 1), y), (peer("x", 3), y)]
        + [(partner, y)]
    )

    f32 = lambda v: v.astype(jnp.float32)
    axes = (("z", "x"), ("x", "z"))
    pos = ((z, x), (x, z))

    def terms_of(h, i, core):
        rows = pl.ds(80 * h, 80)
        return terms.at[i, :, core, rows] if h == 0 else terms.at[:, i, core, rows]

    order = (2, 1, 3, 0)

    def crossing(h, k):
        i = wrap(pos[h][0] + order[k])
        return pltpu.make_async_remote_copy(
            src_ref=terms_of(h, i, 1 - c),
            dst_ref=theirs.at[h, i],
            send_sem=die_send.at[4 * h + k],
            recv_sem=die_recv.at[4 * h + k],
            device_id=(partner, y),
            device_id_type=MESH,
        )

    def both_cores(h, k):
        i = wrap(pos[h][0] + order[k])
        crossing(h, k).wait_recv()
        chip[h, i] = (f32(terms_of(h, i, c)[...]) + f32(theirs[h, i])).astype(jnp.bfloat16)

    for k in range(4):
        for h in (0, 1):
            crossing(h, k).start()

    def remote(i, src, dst, target):
        return pltpu.make_async_remote_copy(
            src_ref=src,
            dst_ref=dst,
            send_sem=send_sem.at[i],
            recv_sem=recv_sem.at[i],
            device_id=(target, y),
            device_id_type=MESH,
        )

    all_hops = []
    first = []
    for h in (0, 1):
        axis = axes[h][0]
        p = pos[h][0]
        up, down = peer(axis, 1), peer(axis, 3)
        to_far, to_up, to_down = wrap(p + 2), wrap(p + 1), wrap(p + 3)
        lo, hi = pl.ds(0, 2), pl.ds(2, 2)
        hops = [
            remote(12 * h + 0, chip.at[h, to_far, lo], far1.at[h, 0], up),
            remote(12 * h + 1, chip.at[h, to_far, hi], far1.at[h, 1], down),
            remote(12 * h + 2, chip.at[h, to_up, hi], near1.at[h, 0, hi], up),
            remote(12 * h + 3, chip.at[h, to_down, lo], near1.at[h, 1, lo], down),
            remote(12 * h + 4, chip.at[h, to_up, lo], near1.at[h, 0, lo], up),
            remote(12 * h + 5, chip.at[h, to_down, hi], near1.at[h, 1, hi], down),
        ]
        first.append((hops, to_up, to_down))
        all_hops += hops
    for k, ready in enumerate(((0, 1), (2,), (3,), ())):
        for h in (0, 1):
            both_cores(h, k)
            for i in ready:
                first[h][0][i].start()
    for h in (0, 1):
        hops, to_up, to_down = first[h]
        lo, hi = pl.ds(0, 2), pl.ds(2, 2)
        hops[0].wait_recv()
        chip[h, to_up, lo] = (f32(chip[h, to_up, lo]) + f32(far1[h, 0])).astype(jnp.bfloat16)
        hops[4].start()
        hops[1].wait_recv()
        chip[h, to_down, hi] = (f32(chip[h, to_down, hi]) + f32(far1[h, 1])).astype(jnp.bfloat16)
        hops[5].start()
    second = []
    for h in (0, 1):
        hops = first[h][0]
        for k in range(2, 6):
            hops[k].wait_recv()
        out1[h] = (f32(chip[h, pos[h][0]]) + f32(near1[h, 0]) + f32(near1[h, 1])).astype(
            jnp.bfloat16
        )
        axis = axes[h][1]
        p = pos[h][1]
        up, down = peer(axis, 1), peer(axis, 3)
        to_far, to_up, to_down = wrap(p + 2), wrap(p + 1), wrap(p + 3)
        lo, hi = pl.ds(0, HD), pl.ds(HD, HD)
        rows = pl.ds(0, 80)
        hops = [
            remote(12 * h + 6, out1.at[h, to_far, rows, lo], far2.at[h, 0], up),
            remote(12 * h + 7, out1.at[h, to_far, rows, hi], far2.at[h, 1], down),
            remote(12 * h + 8, out1.at[h, to_up, rows, hi], pieces.at[h, 1, rows, hi], up),
            remote(12 * h + 9, out1.at[h, to_down, rows, lo], pieces.at[h, 2, rows, lo], down),
            remote(12 * h + 10, out1.at[h, to_up, rows, lo], pieces.at[h, 1, rows, lo], up),
            remote(12 * h + 11, out1.at[h, to_down, rows, hi], pieces.at[h, 2, rows, hi], down),
        ]
        for k in range(4):
            hops[k].start()
        second.append((hops, to_up, to_down))
        all_hops += hops
    for h in (0, 1):
        hops, to_up, to_down = second[h]
        hops[0].wait_recv()
        out1[h, to_up, :, 0:HD] = (f32(out1[h, to_up, :, 0:HD]) + f32(far2[h, 0])).astype(
            jnp.bfloat16
        )
        hops[4].start()
        hops[1].wait_recv()
        out1[h, to_down, :, HD:] = (f32(out1[h, to_down, :, HD:]) + f32(far2[h, 1])).astype(
            jnp.bfloat16
        )
        hops[5].start()
    for h in (0, 1):
        hops = second[h][0]
        for k in range(2, 6):
            hops[k].wait_recv()
        pieces[h, 0] = out1[h, pos[h][1]]
    for hop in all_hops:
        hop.wait_send()
    for h in (0, 1):
        for k in range(4):
            crossing(h, k).wait_send()


def scatter(terms):
    vmem = pl.BlockSpec(memory_space=pltpu.VMEM)
    bf16 = jnp.bfloat16
    width = terms.shape[-1]
    return pl.pallas_call(
        scatter_kernel,
        out_shape=jax.ShapeDtypeStruct((2, 3, 80, width), bf16),
        in_specs=[vmem],
        out_specs=vmem,
        scratch_shapes=[
            pltpu.VMEM((2, 4, 4, 80, width), bf16),
            pltpu.VMEM((2, 4, 4, 80, width), bf16),
            pltpu.VMEM((2, 2, 2, 80, width), bf16),
            pltpu.VMEM((2, 2, 4, 80, width), bf16),
            pltpu.VMEM((2, 4, 80, width), bf16),
            pltpu.VMEM((2, 2, 80, HD), bf16),
            pltpu.SemaphoreType.DMA((8,)),
            pltpu.SemaphoreType.DMA((8,)),
            pltpu.SemaphoreType.DMA((24,)),
            pltpu.SemaphoreType.DMA((24,)),
        ],
        compiler_params=pltpu.CompilerParams(
            collective_id=2, has_side_effects=True, vmem_limit_bytes=VMEM_ALL
        ),
        name="scatter",
    )(terms)


def total_kernel(pieces, grad_k, grad_v):
    for h in (0, 1):
        rows = slice(80 * h, 80 * h + 80)
        total = sum(pieces[h, k].astype(jnp.float32) for k in range(3)).astype(jnp.bfloat16)
        grad_k[rows, :] = total[:, 0:HD]
        grad_v[rows, :] = total[:, HD:]


def total(pieces):
    vmem = pl.BlockSpec(memory_space=pltpu.VMEM)
    return pl.pallas_call(
        total_kernel,
        out_shape=(jax.ShapeDtypeStruct((ROWS, HD), jnp.bfloat16),) * 2,
        in_specs=[vmem],
        out_specs=(vmem, vmem),
        name="total",
    )(pieces)


def body(
    teacher_query,
    teacher_keys,
    teacher_values,
    teacher_docs,
    student_query,
    student_keys,
    student_values,
    student_docs,
    projector,
    teacher_spans,
    student_spans,
):
    gath = gather(teacher_keys, teacher_values, student_keys, student_values)
    gath = gath.reshape(TOKENS, TKV + SKV)
    pooled = forward(teacher_docs, teacher_query, gath, teacher_spans)
    arrived, sctx, qback, weight_sums = align(
        student_docs, pooled, projector, gath, student_keys, student_values, student_query
    )
    grad_q, terms = backward(
        student_docs, qback, gath, sctx, weight_sums, student_query, arrived, student_spans
    )
    grad_k, grad_v = total(scatter(terms.reshape(4, 4, 2, ROWS, 2 * HD)))
    return grad_q, grad_k, grad_v


def solution(mesh):
    return jax.shard_map(
        body,
        mesh=mesh,
        in_specs=(
            P("seq", "mp"),
            P("seq", "mp"),
            P("seq", "mp"),
            P(),
            P("seq", "mp"),
            P("seq", "mp"),
            P("seq", "mp"),
            P(),
            P("mp", None),
            P("seq", None, None),
            P("seq", None, None),
        ),
        out_specs=(P("seq", "mp"), P("seq", "mp"), P("seq", "mp")),
        check_vma=False,
    )
```

time: 125 us -> 116 us (0.928)
  Pallas kernels: 122 us -> 115 us
  local copies, waits for them, and re-layouts: 2.8 us -> 0 us
    pallas_call x3 -> x4, Pallas kernels: 84.6 us -> 76.8 us  [the longest x1 35.8 us: align(): pl.pallas_call(align_kernel, out_shape=(jax.ShapeDtypeStruct((SLOTS, cols...]
    unnamed x2 -> x0, local copies, waits for them, and re-layouts: 2.8 us -> none
where the time goes in v1:
time: 116 us
  Pallas kernels  115 us (99%)
    pallas_call x1, Pallas kernels, align(): pl.pallas_call(align_kernel, out_shape=(jax.ShapeDtypeStruct((SLOTS, cols...  35.8 us
    pallas_call x1, Pallas kernels, scatter(): pl.pallas_call(scatter_kernel, out_shape=jax.ShapeDtypeStruct((2, 3, 80,...  34.4 us
    pallas_call x1, Pallas kernels, gather(): pl.pallas_call(gather_kernel, out_shape=jax.ShapeDtypeStruct((SEQ, ROWS,...  33 us
    pallas_call x1, Pallas kernels, backward(): pl.pallas_call(backward_kernel, out_shape=(jax.ShapeDtypeStruct((ROWS, SR...  5.63 us
    pallas_call x1, Pallas kernels, forward(): pl.pallas_call(forward_kernel, out_shape=jax.ShapeDtypeStruct((SLOTS, TG...  5.09 us

profile of v1, /device:TPU:0, one launch (start us, length us, event | category | flops | bytes accessed | tf_op | source)
XLA Modules:
  0.0 116.2 jit_solution(8546073209861143696)
XLA Ops:
  0.6 33.0 %gather.1 = bf16[32,160,768]{2,1,0:T(8,128)(2,1)} custom-call(bf16[160,256]{1,0:T(8,128)(2,1)} %tk.1, bf16[160,256]{1,0:T(8,128)(2,1)} %tv.1, bf16[160,128]{1,0:T(8,128)(2,1)} %sk.3, bf16[160,128]{1,0:T(8,128)(2,1)} %sv.3), custom_call_target="tpu_custom_call" | custom-call | tf_op jit(solution)/shard_map/gather/pallas_call | solution.py:493
  33.7 5.1 %forward.1.pooled = bf16[128,2048]{1,0:T(8,128)(2,1)} custom-call(s32[16]{0:T(128)} %tdocs.1, bf16[160,2048]{1,0:T(8,128)(2,1)} %tq.1, bf16[5120,768]{1,0:T(8,128)(2,1)} %bitcast.2, s32[1,2,128]{2,1,0:T(2,128)} %tspans.1), custom_call_target="tpu_custom_call" | custom-call | tf_op jit(solution)/shard_map/forward/pallas_call | solution.py:434
  38.8 35.8 %align.1 = (f32[128,896]{1,0:T(8,128)}, bf16[160,896]{1,0:T(8,128)(2,1)}, bf16[1120,256]{1,0:T(8,128)(2,1)}, f32[8,1120]{1,0:T(8,128)}) custom-call(s32[16]{0:T(128)} %sdocs.3, bf16[128,2048]{1,0:T(8,128)(2,1)} %forward.1.pooled, bf16[2048,3584]{1,0:T(8,128)(2,1)} %projector.1, bf16[5120,768]{1,0:T(8,128)(2,1)} %bitcast.3, bf16[160,128]{1,0:T(8,128)(2,1)} %sk.3, ...), custom_call_target="tpu_custom_call" | custom-call | tf_op jit(solution)/shard_map/align/pallas_call | solution.py:653
  74.5 5.6 %backward.1 = (bf16[160,896]{1,0:T(8,128)(2,1)}, bf16[5120,256]{1,0:T(8,128)(2,1)}) custom-call(s32[16]{0:T(128)} %sdocs.3, bf16[1120,256]{1,0:T(8,128)(2,1)} %get-tuple-element.11.qback_in, bf16[5120,768]{1,0:T(8,128)(2,1)} %bitcast.4, bf16[160,896]{1,0:T(8,128)(2,1)} %get-tuple-element.12.sctx_in, f32[8,1120]{1,0:T(8,128)} %get-tuple-element.13.weight_sums, ...), custom_call_target="tpu_custom_call" | custom-call | tf_op jit(solution)/shard_map/backward/pallas_call | solution.py:796
  80.2 34.4 %scatter.1.pieces = bf16[2,3,80,256]{3,2,1,0:T(8,128)(2,1)} custom-call(bf16[4,4,2,160,256]{4,3,2,1,0:T(8,128)(2,1)} %bitcast.5), custom_call_target="tpu_custom_call" | custom-call | tf_op jit(solution)/shard_map/scatter/pallas_call | solution.py:966
  114.6 1.6 %total.1 = (bf16[160,128]{1,0:T(8,128)(2,1)}, bf16[160,128]{1,0:T(8,128)(2,1)}) custom-call(bf16[2,3,80,256]{3,2,1,0:T(8,128)(2,1)} %scatter.1.pieces), custom_call_target="tpu_custom_call" | custom-call | tf_op jit(solution)/shard_map/total/pallas_call | solution.py:1000

commit v2 on v1

--- a/solution.py
+++ b/solution.py
@@ -22,12 +22,13 @@
 NDOCS = 16
 ONES, FLAG = NDOCS, NDOCS + 3
 FAR = 1 << 20
-FB = 512
-BB = 512
+FB = 768
+BB = 768
 SB = 640
+STEPS = -(-TOKENS // FB)
 TKV, SKV = 2 * TG * HD, 2 * HD
 CHUNK = 1280
-VMEM_ALL = 60 * 1024 * 1024
+MIB = 1 << 20
 
 NT = (((1,), (1,)), ((), ()))
 TN = (((0,), (0,)), ((), ()))
@@ -300,10 +301,17 @@
 
     def start(self):
         self.own_copy().start()
-
+        self.start_blocks()
+
+    def start_blocks(self):
         @pl.loop(0, self.steps)
         def _(step):
             self.copy(step).start()
+
+    def wait_blocks(self):
+        @pl.loop(0, self.steps)
+        def _(step):
+            self.copy(step).wait()
 
     def marks(self, step):
         return key_marks(
@@ -439,13 +447,13 @@
         scratch_shapes=[
             pltpu.VMEM((TG, tw, 2 * HD), bf16),
             pltpu.VMEM((ROWS, 2 * TG * HD), bf16),
-            pltpu.VMEM((TOKENS // FB, FB, 2 * TG * HD), bf16),
+            pltpu.VMEM((STEPS, FB, 2 * TG * HD), bf16),
             pltpu.VMEM((TG, HD + 16, tw), f32),
             pltpu.VMEM((TG, 1, tw), f32),
             pltpu.SemaphoreType.DMA,
-            pltpu.SemaphoreType.DMA((TOKENS // FB,)),
+            pltpu.SemaphoreType.DMA((STEPS,)),
         ],
-        compiler_params=pltpu.CompilerParams(vmem_limit_bytes=VMEM_ALL),
+        compiler_params=pltpu.CompilerParams(vmem_limit_bytes=34 * MIB),
         name="forward",
     )(tdocs, tq, gath, tspans)
 
@@ -501,7 +509,7 @@
             pltpu.SemaphoreType.DMA((GATHER_OPS,)),
         ],
         compiler_params=pltpu.CompilerParams(
-            collective_id=0, has_side_effects=True, vmem_limit_bytes=VMEM_ALL
+            collective_id=0, has_side_effects=True, vmem_limit_bytes=12 * MIB
         ),
         name="gather",
     )(tk, tv, sk, sv)
@@ -680,7 +688,7 @@
             pltpu.SemaphoreType.DMA((2,)),
         ],
         compiler_params=pltpu.CompilerParams(
-            collective_id=1, has_side_effects=True, vmem_limit_bytes=VMEM_ALL
+            collective_id=1, has_side_effects=True, vmem_limit_bytes=38 * MIB
         ),
         name="align",
     )(sdocs, pooled, projector, gath, sk, sv, sq)
@@ -696,17 +704,15 @@
     sctx[...] = sctx_in[...]
     window.own_copy().wait()
 
-    @pl.loop(0, window.steps)
-    def _(step):
-        window.copy(step).wait()
-
     @pl.when(too_large(weight_sums[...]))
     def _():
+        window.wait_blocks()
         stack_heads(stack, sq, 0, SR)
         mark_queries(stack, own.at[:, 0:HD], window.place, window.lanes, SR)
         attention = Attention([stack], sums, acc, top, SR)
         attention.safe_window(window)
         student_results(attention, stack, window.lanes, sctx, qback)
+        window.start_blocks()
 
     width = SR * ROWS
     terms[...] = jnp.zeros(terms.shape, terms.dtype)
@@ -775,6 +781,7 @@
 
     @pl.loop(0, window.steps)
     def _(step):
+        window.copy(step).wait()
         block(window.blocks.at[step], window.marks(step), window.at(step), False)
 
     for h in range(SR):
@@ -805,7 +812,7 @@
             pltpu.VMEM((sw, 2 * HD), bf16),
             pltpu.VMEM((HD, sw), jnp.float32),
             pltpu.VMEM((ROWS, 2 * HD), bf16),
-            pltpu.VMEM((TOKENS // BB, BB, 2 * HD), bf16),
+            pltpu.VMEM((STEPS, BB, 2 * HD), bf16),
             pltpu.VMEM((sw, 2 * HD), bf16),
             pltpu.VMEM((ROWS, SR * HD), bf16),
             pltpu.VMEM((sw, 2 * HD), bf16),
@@ -813,16 +820,16 @@
             pltpu.VMEM((1, HD + 16, sw), jnp.float32),
             pltpu.VMEM((1, 1, sw), jnp.float32),
             pltpu.SemaphoreType.DMA,
-            pltpu.SemaphoreType.DMA((TOKENS // BB,)),
+            pltpu.SemaphoreType.DMA((STEPS,)),
         ],
-        compiler_params=pltpu.CompilerParams(vmem_limit_bytes=VMEM_ALL),
+        compiler_params=pltpu.CompilerParams(vmem_limit_bytes=34 * MIB),
         name="backward",
     )(sdocs, qback, gath, sctx, weight_sums, sq, arrived, sspans)
 
 
 def scatter_kernel(
-    terms, pieces, theirs, chip, far1, near1, out1, far2,
-    die_send, die_recv, send_sem, recv_sem,
+    terms, pieces, theirs, ours, chip, far1, near1, out1, far2,
+    die_send, die_recv, own_sem, send_sem, recv_sem,
 ):
     me, z, x, c = place()
     y = lax.axis_index("mp")
@@ -832,20 +839,30 @@
     def peer(axis, d):
         return seq_of(wrap(z + d), x, c) if axis == "z" else seq_of(z, wrap(x + d), c)
 
+    f32 = lambda v: v.astype(jnp.float32)
+    axes = (("z", "x"), ("x", "z"))
+    pos = ((z, x), (x, z))
+
+    def terms_of(h, i, core):
+        rows = pl.ds(80 * h, 80)
+        return terms.at[i, :, core, rows] if h == 0 else terms.at[:, i, core, rows]
+
+    order = (2, 1, 3, 0)
+
+    def own_copy(h, k):
+        i = wrap(pos[h][0] + order[k])
+        return pltpu.make_async_copy(
+            terms_of(h, i, c), ours.at[h, i], own_sem.at[4 * h + k]
+        )
+
+    for k in range(4):
+        for h in (0, 1):
+            own_copy(h, k).start()
+
     greet(
         [(peer("z", 1), y), (peer("z", 3), y), (peer("x", 1), y), (peer("x", 3), y)]
         + [(partner, y)]
     )
-
-    f32 = lambda v: v.astype(jnp.float32)
-    axes = (("z", "x"), ("x", "z"))
-    pos = ((z, x), (x, z))
-
-    def terms_of(h, i, core):
-        rows = pl.ds(80 * h, 80)
-        return terms.at[i, :, core, rows] if h == 0 else terms.at[:, i, core, rows]
-
-    order = (2, 1, 3, 0)
 
     def crossing(h, k):
         i = wrap(pos[h][0] + order[k])
@@ -860,8 +877,9 @@
 
     def both_cores(h, k):
         i = wrap(pos[h][0] + order[k])
+        own_copy(h, k).wait()
         crossing(h, k).wait_recv()
-        chip[h, i] = (f32(terms_of(h, i, c)[...]) + f32(theirs[h, i])).astype(jnp.bfloat16)
+        chip[h, i] = (f32(ours[h, i]) + f32(theirs[h, i])).astype(jnp.bfloat16)
 
     for k in range(4):
         for h in (0, 1):
@@ -966,9 +984,10 @@
     return pl.pallas_call(
         scatter_kernel,
         out_shape=jax.ShapeDtypeStruct((2, 3, 80, width), bf16),
-        in_specs=[vmem],
+        in_specs=[pl.BlockSpec(memory_space=pl.ANY)],
         out_specs=vmem,
         scratch_shapes=[
+            pltpu.VMEM((2, 4, 4, 80, width), bf16),
             pltpu.VMEM((2, 4, 4, 80, width), bf16),
             pltpu.VMEM((2, 4, 4, 80, width), bf16),
             pltpu.VMEM((2, 2, 2, 80, width), bf16),
@@ -977,11 +996,12 @@
             pltpu.VMEM((2, 2, 80, HD), bf16),
             pltpu.SemaphoreType.DMA((8,)),
             pltpu.SemaphoreType.DMA((8,)),
+            pltpu.SemaphoreType.DMA((8,)),
             pltpu.SemaphoreType.DMA((24,)),
             pltpu.SemaphoreType.DMA((24,)),
         ],
         compiler_params=pltpu.CompilerParams(
-            collective_id=2, has_side_effects=True, vmem_limit_bytes=VMEM_ALL
+            collective_id=2, has_side_effects=True, vmem_limit_bytes=18 * MIB
         ),
         name="scatter",
     )(terms)
@@ -1002,6 +1022,7 @@
         out_shape=(jax.ShapeDtypeStruct((ROWS, HD), jnp.bfloat16),) * 2,
         in_specs=[vmem],
         out_specs=(vmem, vmem),
+        compiler_params=pltpu.CompilerParams(vmem_limit_bytes=8 * MIB),
         name="total",
     )(pieces)
 
@@ -1019,7 +1040,12 @@
     teacher_spans,
     student_spans,
 ):
-    gath = gather(teacher_keys, teacher_values, student_keys, student_values)
+    gath = gather(
+        *(
+            pltpu.with_memory_space_constraint(x, pltpu.HBM)
+            for x in (teacher_keys, teacher_values, student_keys, student_values)
+        )
+    )
     gath = gath.reshape(TOKENS, TKV + SKV)
     pooled = forward(teacher_docs, teacher_query, gath, teacher_spans)
     arrived, sctx, qback, weight_sums = align(

time: 116 us -> 102 us (0.88)
  Pallas kernels: 115 us -> 102 us
    pallas_call x1, Pallas kernels: 33 us -> 29.9 us  [gather(): pl.pallas_call(gather_kernel, out_shape=jax.ShapeDtypeStruct((SEQ, ROWS,...]
    pallas_call x1, Pallas kernels: 34.4 us -> 31.5 us  [scatter(): pl.pallas_call(scatter_kernel, out_shape=jax.ShapeDtypeStruct((2, 3, 80,...]
    pallas_call x1, Pallas kernels: 35.8 us -> 33.2 us  [align(): pl.pallas_call(align_kernel, out_shape=(jax.ShapeDtypeStruct((SLOTS, cols...]
    pallas_call x1, Pallas kernels: 5.63 us -> 3.3 us  [backward(): pl.pallas_call(backward_kernel, out_shape=(jax.ShapeDtypeStruct((ROWS, SR...]
    pallas_call x1, Pallas kernels: 5.09 us -> 2.9 us  [forward(): pl.pallas_call(forward_kernel, out_shape=jax.ShapeDtypeStruct((SLOTS, TG...]
where the time goes in v2:
time: 102 us
  Pallas kernels  102 us (100%)
    pallas_call x1, Pallas kernels, align(): pl.pallas_call(align_kernel, out_shape=(jax.ShapeDtypeStruct((SLOTS, cols...  33.2 us
    pallas_call x1, Pallas kernels, scatter(): pl.pallas_call(scatter_kernel, out_shape=jax.ShapeDtypeStruct((2, 3, 80,...  31.5 us
    pallas_call x1, Pallas kernels, gather(): pl.pallas_call(gather_kernel, out_shape=jax.ShapeDtypeStruct((SEQ, ROWS,...  29.9 us
    pallas_call x1, Pallas kernels, backward(): pl.pallas_call(backward_kernel, out_shape=(jax.ShapeDtypeStruct((ROWS, SR...  3.3 us
    pallas_call x1, Pallas kernels, forward(): pl.pallas_call(forward_kernel, out_shape=jax.ShapeDtypeStruct((SLOTS, TG...  2.9 us

profile of v2, /device:TPU:0, one launch (start us, length us, event | category | flops | bytes accessed | tf_op | source)
XLA Modules:
  0.0 102.4 jit_solution(54680865072505804)
XLA Ops:
  0.6 0.0 copy-start.4
  0.6 0.0 copy-start.3
  0.7 0.0 copy-start.2
  0.7 0.0 copy-start
  0.7 0.0 copy-start.5
  0.7 0.0 copy-start.7
  0.7 0.0 copy-start.1
  0.7 29.9 %gather.1 = bf16[32,160,768]{2,1,0:T(8,128)(2,1)S(1)} custom-call(bf16[160,256]{1,0:T(8,128)(2,1)} %tk.1, bf16[160,256]{1,0:T(8,128)(2,1)} %tv.1, bf16[160,128]{1,0:T(8,128)(2,1)} %sk.3, bf16[160,128]{1,0:T(8,128)(2,1)} %sv.3), custom_call_target="tpu_custom_call" | custom-call | tf_op jit(solution)/shard_map/gather/pallas_call | solution.py:501
  30.7 0.0 copy-done.5
  30.7 0.0 copy-done.7
  30.7 0.0 copy-done.1
  30.7 2.9 %forward.1.pooled = bf16[128,2048]{1,0:T(8,128)(2,1)S(1)} custom-call(s32[16]{0:T(128)S(1)} %copy-done.7, bf16[160,2048]{1,0:T(8,128)(2,1)S(1)} %copy-done.1, bf16[5120,768]{1,0:T(8,128)(2,1)S(1)} %bitcast.2, s32[1,2,128]{2,1,0:T(2,128)S(1)} %copy-done.5), custom_call_target="tpu_custom_call" | custom-call | tf_op jit(solution)/shard_map/forward/pallas_call | solution.py:442
  33.6 0.0 copy-done.4
  33.6 0.0 copy-done.3
  33.6 0.0 copy-done.2
  33.6 0.0 copy-done
  33.6 0.0 copy-start.6
  33.6 33.2 %align.1 = (f32[128,896]{1,0:T(8,128)S(1)}, bf16[160,896]{1,0:T(8,128)(2,1)S(1)}, bf16[1120,256]{1,0:T(8,128)(2,1)S(1)}, f32[8,1120]{1,0:T(8,128)S(1)}) custom-call(s32[16]{0:T(128)S(1)} %copy-done.4, bf16[128,2048]{1,0:T(8,128)(2,1)S(1)} %forward.1.pooled, bf16[2048,3584]{1,0:T(8,128)(2,1)} %projector.1, bf16[5120,768]{1,0:T(8,128)(2,1)S(1)} %bitcast.3, ...), custom_call_target="tpu_custom_call" | custom-call | tf_op jit(solution)/shard_map/align/pallas_call | solution.py:661
  66.9 0.0 copy-done.6
  66.9 3.3 %backward.1 = (bf16[160,896]{1,0:T(8,128)(2,1)}, bf16[5120,256]{1,0:T(8,128)(2,1)S(1)}) custom-call(s32[16]{0:T(128)S(1)} %copy-done.4, bf16[1120,256]{1,0:T(8,128)(2,1)S(1)} %get-tuple-element.11.qback_in, bf16[5120,768]{1,0:T(8,128)(2,1)S(1)} %bitcast.4, bf16[160,896]{1,0:T(8,128)(2,1)S(1)} %get-tuple-element.12.sctx_in, ...), custom_call_target="tpu_custom_call" | custom-call | tf_op jit(solution)/shard_map/backward/pallas_call | solution.py:803
  70.2 31.5 %scatter.1.pieces = bf16[2,3,80,256]{3,2,1,0:T(8,128)(2,1)S(1)} custom-call(bf16[4,4,2,160,256]{4,3,2,1,0:T(8,128)(2,1)S(1)} %bitcast.5), custom_call_target="tpu_custom_call" | custom-call | tf_op jit(solution)/shard_map/scatter/pallas_call | solution.py:984
  101.7 0.7 total.1
Async XLA Ops:
  0.6 33.0 %copy-start.4 = (s32[16]{0:T(128)S(1)}, s32[16]{0:T(128)}, u32[]{:S(2)}) copy-start(s32[16]{0:T(128)} %sdocs.3) | copy-start | bytes 196
  0.6 33.0 %copy-start.3 = (bf16[160,128]{1,0:T(8,128)(2,1)S(1)}, bf16[160,128]{1,0:T(8,128)(2,1)}, u32[]{:S(2)}) copy-start(bf16[160,128]{1,0:T(8,128)(2,1)} %sv.3) | copy-start | bytes 122884
  0.7 33.0 %copy-start.2 = (bf16[160,128]{1,0:T(8,128)(2,1)S(1)}, bf16[160,128]{1,0:T(8,128)(2,1)}, u32[]{:S(2)}) copy-start(bf16[160,128]{1,0:T(8,128)(2,1)} %sk.3) | copy-start | bytes 122884
  0.7 33.0 %copy-start = (bf16[160,896]{1,0:T(8,128)(2,1)S(1)}, bf16[160,896]{1,0:T(8,128)(2,1)}, u32[]{:S(2)}) copy-start(bf16[160,896]{1,0:T(8,128)(2,1)} %sq.3) | copy-start | bytes 860164
  0.7 30.0 %copy-start.5 = (s32[1,2,128]{2,1,0:T(2,128)S(1)}, s32[1,2,128]{2,1,0:T(2,128)}, u32[]{:S(2)}) copy-start(s32[1,2,128]{2,1,0:T(2,128)} %tspans.1) | copy-start | bytes 3076
  0.7 30.0 %copy-start.7 = (s32[16]{0:T(128)S(1)}, s32[16]{0:T(128)}, u32[]{:S(2)}) copy-start(s32[16]{0:T(128)} %tdocs.1) | copy-start | bytes 196
  0.7 30.0 %copy-start.1 = (bf16[160,2048]{1,0:T(8,128)(2,1)S(1)}, bf16[160,2048]{1,0:T(8,128)(2,1)}, u32[]{:S(2)}) copy-start(bf16[160,2048]{1,0:T(8,128)(2,1)} %tq.1) | copy-start | bytes 1966084
  33.6 33.2 %copy-start.6 = (s32[1,2,128]{2,1,0:T(2,128)S(1)}, s32[1,2,128]{2,1,0:T(2,128)}, u32[]{:S(2)}) copy-start(s32[1,2,128]{2,1,0:T(2,128)} %sspans.1) | copy-start | bytes 3076
